TPU v7x, 32 devices: a whole 2x2x4 slice. The times are simulated.
32 devices in a mesh: member: 4 (over x, core), region: 8 (over z, y).
Axes of the slice: x: 2, y: 2, z: 4, core: 2. Of those that a mesh axis runs over, the one named last changes fastest.
Arguments:
- background: bfloat16 [4, 8, 96, 256, 64], P(None, 'region', None, 'member'), may hold values from -6 to 6
- obs_ensemble: bfloat16 [4, 8, 1, 256, 1024], P(None, 'region', None, 'member'), may hold values from -6 to 6
- obs_value: float32 [4, 8, 1, 1024], P('member', 'region'), may hold values from -12 to 12
- obs_weight: float32 [4, 8, 1, 1024], P('member', 'region'), may hold values from 0.05 to 1
- stencil: int32 [4, 8, 4, 64], P('member', 'region'), may hold values from 0 to 31, as said below
- stencil_weight: float32 [4, 8, 4, 64], P('member', 'region'), may hold values from 0.05 to 1
- block_target: int32 [4, 8, 8], replicated, may hold values from 0 to 255, as said below
Outputs:
- analysis: float32 [8, 96, 256, 256], P('region', None, 'member')
Inputs may be any that keep to these rules, and one draw needn't show every extreme that they name: `stencil`: each entry names a coarse point whose band and patch each differ by at most one from those of its column. `block_target`: A permutation of all blocks. The 8 blocks of one band in one patch go to distinct owners (owner = value // 32); the blocks of one patch go to any owner at most 4 at a time, and exactly 4 to some owner.
All inputs are finite; a program needn't handle non-finite values.
Results may differ from a plain program's by a relative error of at most 0.0003.
Values may be sent and summed in bfloat16 or wider, within the bound.
No kernel may reach another device: no remote copies, remote signals or barrier semaphores. Data moves between devices by JAX's collectives and lax.ppermute only.
A program may use at most 128 MiB of HBM per device.

v0:
```python
import functools

import jax
import jax.numpy as jnp
from jax import lax
from jax.experimental import pallas as pl
from jax.experimental.pallas import tpu as pltpu
from jax.sharding import PartitionSpec as P

SWEEPS = 8
LANES = 128
CODE_TOP = 32700.0
LOG2E = 1.4426950408889634


largest_value = lax.Precision.HIGHEST
three_pass = lax.Precision.HIGH


def with_halo(block, sides, width):
    for axis, dim in sides:
        count = lax.axis_size(axis)
        forward = [(i, i + 1) for i in range(count - 1)]
        backward = [(target, source) for source, target in forward]
        low = lax.ppermute(
            lax.slice_in_dim(block, block.shape[dim] - width, None, axis=dim), axis, forward
        )
        high = lax.ppermute(lax.slice_in_dim(block, 0, width, axis=dim), axis, backward)
        block = jnp.concatenate([low, block, high], axis=dim)
    return block


def band_members(pieces, axis):
    count = lax.axis_size(axis)
    here = lax.axis_index(axis)
    arrived = []
    for step in range(count - 1, 0, -1):
        piece = lax.dynamic_index_in_dim(pieces, (here + step) % count, 0, keepdims=False)
        ring = [(i, (i + step) % count) for i in range(count)]
        arrived.append(lax.ppermute(piece, axis, ring))
    arrived.append(lax.dynamic_index_in_dim(pieces, here, 0, keepdims=False))
    width = arrived[0].shape[1]
    ringed = jnp.concatenate(arrived + arrived, axis=1)
    return lax.dynamic_slice_in_dim(ringed, (count - 1 - here) * width, count * width, axis=1)


def build_transforms(obs_pert, departure, obs_weight):
    scaled = obs_pert * obs_weight[:, None, :]
    gram_matrix = jnp.einsum("nko,nlo->nkl", scaled, obs_pert, precision=largest_value)
    forcing = jnp.einsum("nko,no->nk", scaled, departure, precision=largest_value)
    members = gram_matrix.shape[-1]
    identity = jnp.eye(members, dtype=jnp.float32)
    system = gram_matrix + (members - 1.0) * identity
    norm_sum = jnp.sqrt(jnp.sum(system * system, axis=(1, 2)))
    iterate = system / norm_sum[:, None, None]
    inverse = jnp.broadcast_to(identity, system.shape)
    for _ in range(SWEEPS):
        factor = 1.5 * identity - 0.5 * jnp.matmul(inverse, iterate, precision=three_pass)
        iterate = jnp.matmul(iterate, factor, precision=three_pass)
        inverse = jnp.matmul(factor, inverse, precision=three_pass)
    first_pass = jnp.einsum("nkl,nl->nk", inverse, forcing, precision=largest_value)
    mean_weight = (
        jnp.einsum("nkl,nl->nk", inverse, first_pass, precision=largest_value) / norm_sum[:, None]
    )
    spread = jnp.sqrt((members - 1.0) / norm_sum)[:, None, None] * inverse
    return spread + mean_weight[:, :, None]


def code_scale(exponent):
    return jnp.exp2(exponent) * (1.0 / CODE_TOP)


def column_kernel(
    from_ref, slot_ref, share_ref, states_ref, table_ref, out_ref, rows_ref, mix_ref, wide_ref,
    *, member_count, block_size, levels, members,
):
    owner = pl.program_id(0)
    first_column = from_ref[owner] * block_size
    width = members // member_count
    folds = max(1, LANES // width)
    rows = levels // folds
    rows_ref[...] = states_ref[...].astype(jnp.float32).reshape(members * block_size, levels)
    lane_group = lax.broadcasted_iota(jnp.int32, (rows, LANES), 1) // width
    strip = 64
    for i in range(block_size):
        column = first_column + i
        slots = [slot_ref[s, column] for s in range(4)]
        shares = [share_ref[s, column] for s in range(4)]
        buffer = i % 2
        for r in range(0, members, strip):
            mixed = shares[0] * table_ref[slots[0], r : r + strip, :]
            for s in range(1, 4):
                mixed = mixed + shares[s] * table_ref[slots[s], r : r + strip, :]
            high = mixed.astype(jnp.bfloat16)
            low = (mixed - high.astype(jnp.float32)).astype(jnp.bfloat16)
            mix_ref[buffer, r : r + strip, :members] = high
            mix_ref[buffer, r : r + strip, members:] = low
        state = rows_ref[pl.ds(i, members, stride=block_size), :].astype(jnp.bfloat16)
        both = lax.dot_general(
            state, mix_ref[buffer], (((0,), (0,)), ((), ())), preferred_element_type=jnp.float32
        )
        fresh = both[:, :members] + both[:, members:]
        for m in range(member_count):
            tile, offset = divmod(m * width, LANES)
            joined = None
            for h in range(folds):
                piece = fresh[h * rows : (h + 1) * rows, tile * LANES : (tile + 1) * LANES]
                shift = (h * width - offset) % LANES
                if shift:
                    piece = pltpu.roll(piece, shift, 1)
                joined = piece if joined is None else jnp.where(lane_group == h, piece, joined)
            wide_ref[m, pl.ds(i, rows, stride=block_size), :] = joined
    for m in range(member_count):
        values = wide_ref[m].reshape(rows, block_size, LANES)
        top = jnp.max(jnp.abs(values), axis=0)
        exponent = jnp.clip(jnp.ceil(jnp.log(top) * LOG2E), -100.0, 100.0)
        code = jnp.round(values * (1.0 / code_scale(exponent))[None])
        code = code.astype(jnp.int32).reshape(rows * block_size, LANES)
        out_ref[m, 0, : rows * block_size, :] = code.astype(jnp.int16)
        tail = jnp.concatenate([exponent, exponent], axis=0).astype(jnp.int32)
        out_ref[m, 0, rows * block_size :, :] = tail.astype(jnp.int16)


def columns_to_blocks(states, table, slots, share, send_from, member_count, block_size):
    members, columns, levels = states.shape
    patches = send_from.shape[0]
    width = members // member_count
    folds = max(1, LANES // width)
    rows = levels // folds
    coded = (rows + 2) * block_size
    kernel = functools.partial(
        column_kernel, member_count=member_count, block_size=block_size, levels=levels,
        members=members,
    )
    return pl.pallas_call(
        kernel,
        grid_spec=pltpu.PrefetchScalarGridSpec(
            num_scalar_prefetch=3,
            grid=(patches,),
            in_specs=[
                pl.BlockSpec((members, block_size, levels), lambda o, f, a, b: (0, f[o], 0)),
                pl.BlockSpec(table.shape, lambda o, f, a, b: (0, 0, 0)),
            ],
            out_specs=pl.BlockSpec(
                (member_count, 1, coded, LANES), lambda o, f, a, b: (0, o, 0, 0)
            ),
            scratch_shapes=[
                pltpu.VMEM((members * block_size, levels), jnp.float32),
                pltpu.VMEM((2, members, 2 * members), jnp.bfloat16),
                pltpu.VMEM((member_count, rows * block_size, LANES), jnp.float32),
            ],
        ),
        out_shape=jax.ShapeDtypeStruct((member_count, patches, coded, LANES), jnp.int16),
        cost_estimate=pl.CostEstimate(
            flops=4 * columns * levels * members * members, transcendentals=0,
            bytes_accessed=4 * states.size,
        ),
        name="columns",
    )(send_from, slots, share, states, table)


def native_kernel(source_ref, code_ref, tail_ref, out_ref, scale_ref, *, places, block_size):
    folds, pair, width, _ = out_ref.shape

    @pl.when(pl.program_id(0) == 0)
    def _():
        for t in range(places):
            tail = tail_ref[source_ref[t]].astype(jnp.int32).astype(jnp.float32)
            scale_ref[t] = code_scale(tail[:block_size])

    pieces = []
    for t in range(places):
        codes = code_ref[source_ref[t]].astype(jnp.int32).astype(jnp.float32)
        pieces.append((codes, scale_ref[t]))
    for r in range(pair):
        stacked = jnp.concatenate(
            [c[r * block_size : (r + 1) * block_size] * scale for c, scale in pieces], axis=0
        )
        out_ref[:, r] = stacked.T.reshape(folds, width, places * block_size)


def blocks_to_native(incoming, arrive_from, width, levels, block_size):
    sources, _, _ = incoming.shape
    places = arrive_from.shape[0]
    folds = max(1, LANES // width)
    rows = levels // folds
    pair = 2
    return pl.pallas_call(
        functools.partial(native_kernel, places=places, block_size=block_size),
        grid_spec=pltpu.PrefetchScalarGridSpec(
            num_scalar_prefetch=1,
            grid=(rows // pair,),
            in_specs=[
                pl.BlockSpec((sources, pair * block_size, LANES), lambda g, a: (0, g, 0)),
                pl.BlockSpec((sources, 2 * block_size, LANES), lambda g, a: (0, 0, 0)),
            ],
            out_specs=pl.BlockSpec(
                (folds, pair, width, places * block_size), lambda g, a: (0, g, 0, 0)
            ),
            scratch_shapes=[pltpu.VMEM((places, block_size, LANES), jnp.float32)],
        ),
        out_shape=jax.ShapeDtypeStruct((folds, rows, width, places * block_size), jnp.float32),
        name="native",
    )(arrive_from, incoming, incoming[:, rows * block_size :])


def analysis_shards(
    background, obs_ensemble, obs_value, obs_weight, stencil, stencil_weight, block_target
):
    own_obs = band_members(obs_ensemble[:, 0], "member")
    states = lax.all_to_all(
        background[:, 0].transpose(0, 2, 3, 1), "member", split_axis=0, concat_axis=0,
        tiled=True,
    )
    group = own_obs.astype(jnp.float32)
    obs_mean = jnp.mean(group, axis=1)
    transform = build_transforms(
        group - obs_mean[:, None, :], obs_value[0, 0] - obs_mean, obs_weight[0, 0]
    )
    points = transform.shape[0]
    members = transform.shape[1]
    transform = transform + (1.0 - jnp.sum(transform, axis=1, keepdims=True)) / members
    nearby = with_halo(transform[None, None], (("region", 1), ("member", 0)), 1)
    nearby = nearby.reshape(9 * points, members, members)
    columns, levels = states.shape[2:]
    states = states.reshape(members, columns, levels)
    band_index = lax.axis_index("member")
    patch_index = lax.axis_index("region")
    patch_list = lax.axis_size("region")
    member_count = lax.axis_size("member")
    shard_width = members // member_count
    stencil_rows = stencil[0, 0]
    near_band = stencil_rows // (patch_list * points)
    near_patch = stencil_rows // points % patch_list
    local_index = (
        (near_band - band_index + 1) * 3 + (near_patch - patch_index + 1)
    ) * points + stencil_rows % points
    share = stencil_weight[0, 0] / jnp.sum(stencil_weight[0, 0], axis=0, keepdims=True)
    band_count = block_target.shape[0]
    per_device = block_target.shape[2]
    per_owner = band_count * per_device
    block_size = columns // per_device
    owners = block_target // per_owner
    places = block_target % per_owner
    patch_ids = jnp.arange(patch_list, dtype=jnp.int32)
    place_ids = jnp.arange(per_owner, dtype=jnp.int32)
    band_owners = lax.dynamic_index_in_dim(owners, band_index, 0, keepdims=False)
    my_owners = lax.dynamic_index_in_dim(band_owners, patch_index, 0, keepdims=False)
    block_ids = jnp.arange(per_device, dtype=jnp.int32)
    send_hit = my_owners[None, :] == patch_ids[:, None]
    send_from = jnp.sum(send_hit.astype(jnp.int32) * block_ids[None, :], axis=1)
    band_ids = jnp.arange(band_count, dtype=jnp.int32)
    source = band_ids[:, None, None] * patch_list + patch_ids[None, :, None] + 0 * places
    arrive_hit = (owners == patch_index)[None] & (places[None] == place_ids[:, None, None, None])
    arrive_from = jnp.sum(arrive_hit.astype(jnp.int32) * source[None], axis=(1, 2, 3))
    outgoing = columns_to_blocks(
        states, nearby, local_index, share, send_from, member_count, block_size
    )
    outgoing = outgoing.reshape(member_count * patch_list, *outgoing.shape[2:])
    incoming = lax.all_to_all(
        outgoing, ("member", "region"), split_axis=0, concat_axis=0, tiled=True
    )
    native = blocks_to_native(incoming, arrive_from, shard_width, levels, block_size)
    return native.reshape(1, levels, shard_width, per_owner * block_size)


def solution(mesh):
    in_specs = (
        P(None, "region", None, "member", None),
        P(None, "region", None, "member", None),
        P("member", "region", None, None),
        P("member", "region", None, None),
        P("member", "region", None, None),
        P("member", "region", None, None),
        P(),
    )
    out_specs = P("region", None, "member", None)
    return jax.shard_map(analysis_shards, mesh=mesh, in_specs=in_specs, out_specs=out_specs, check_vma=False)
```

profile of v0, /device:TPU:0, one launch (start us, length us, event | category | flops | bytes accessed | tf_op | source)
XLA Modules:
  0.0 214.6 jit_solution(2317706402018621556)
XLA Ops:
  0.0 1.1 dynamic-slice_bitcast_fusion
  1.1 2.5 %collective-permute-start = (bf16[1,64,1024]{2,1,0:T(8,128)(2,1)S(1)}, bf16[1,64,1024]{2,1,0:T(8,128)(2,1)S(1)}, u32[]{:S(2)}, u32[]{:S(2)}) collective-permute-start(bf16[1,64,1024]{2,1,0:T(8,128)(2,1)S(1)} %get-tuple-element.9), channel_id=1, source_target_pairs={{0,24},{8,0},{16,8},{24,16},{1,25},{9,1},{17,9},{25,17},{2,26},{10... | collective-permute-start | bytes 393224 | tf_op jit(solution)/shard_map/ppermute | solution.py:40
  3.5 0.6 collective-permute-start.1
  4.2 5.0 %all-to-all-start = ((bf16[4,64,64,96]{3,2,1,0:T(8,128)(2,1)}), bf16[4,64,64,96]{3,2,1,0:T(8,128)(2,1)}, u32[]{:S(2)}, u32[]{:S(2)}) async-start(bf16[4,64,64,96]{3,2,1,0:T(8,128)(2,1)} %bitcast.111), calls=%async_computation | async-start | bytes 8388608 | tf_op jit(solution)/shard_map/all_to_all | solution.py:211
  9.1 0.0 copy-start.5
  9.1 0.4 collective-permute-start.2
  9.6 0.0 collective-permute-done
  9.6 0.0 collective-permute-done.1
  9.7 49.0 %collective-permute-done.2 = bf16[1,64,1024]{2,1,0:T(8,128)(2,1)S(1)} collective-permute-done((bf16[1,64,1024]{2,1,0:T(8,128)(2,1)S(1)}, bf16[1,64,1024]{2,1,0:T(8,128)(2,1)S(1)}, u32[]{:S(2)}, u32[]{:S(2)}) %collective-permute-start.2) | collective-permute-done | bytes 131104 | tf_op jit(solution)/shard_map/ppermute | solution.py:40
  58.8 0.1 convert_reduce_fusion
  58.9 1.8 multiply_reduce_fusion
  61.4 0.2 fusion.9
  61.6 0.3 fusion.23
  61.9 0.2 fusion.20
  62.1 0.3 fusion.8
  62.4 0.3 fusion.41
  62.7 0.3 fusion.40
  63.0 0.3 fusion.7
  63.3 0.3 fusion.43
  63.5 0.3 fusion.42
  63.8 0.3 fusion.6
  64.1 0.3 fusion.45
  64.4 0.3 fusion.44
  64.7 0.3 fusion.5
  64.9 0.3 fusion.47
  65.2 0.3 fusion.46
  65.5 0.3 fusion.4
  65.8 0.3 fusion.49
  66.1 0.0 copy-start.6
  66.1 0.3 fusion.48
  66.3 0.3 fusion.3
  66.6 0.3 fusion.50
  66.9 0.0 copy-start.3
  66.9 0.3 fusion.51
  67.2 0.3 fusion.2
  67.5 0.0 copy-start.2
  67.5 0.0 copy-start.4
  67.5 0.3 fusion.52
  67.8 1.0 convolution_bitcast_fusion
  68.8 0.3 convolution_bitcast_fusion.1
  69.0 0.3 fusion.53
  69.5 0.1 fusion.21
  69.7 0.1 add_bitcast_fusion
  69.8 1.3 collective-permute-start.4
  71.1 4.6 %collective-permute-start.3 = (f32[1,1,1,256,256]{4,3,2,1,0:T(8,128)S(1)}, f32[1,1,1,256,256]{4,3,2,1,0:T(8,128)S(1)}, u32[]{:S(2)}, u32[]{:S(2)}) collective-permute-start(f32[1,1,1,256,256]{4,3,2,1,0:T(8,128)S(1)} %add_bitcast_fusion), channel_id=1, source_target_pairs={{0,1},{1,2},{2,3},{3,4},{4,5},{5,6},{6,7},{8,9},{9,10},{10,11},{11... | collective-permute-start | bytes 786440 | tf_op jit(solution)/shard_map/ppermute | solution.py:25
  75.7 2.4 %collective-permute-done.4 = f32[1,1,1,256,256]{4,3,2,1,0:T(8,128)S(1)} collective-permute-done((f32[1,1,1,256,256]{4,3,2,1,0:T(8,128)S(1)}, f32[1,1,1,256,256]{4,3,2,1,0:T(8,128)S(1)}, u32[]{:S(2)}, u32[]{:S(2)}) %collective-permute-start.4) | collective-permute-done | bytes 262176 | tf_op jit(solution)/shard_map/ppermute | solution.py:28
  78.0 5.4 %collective-permute-done.3 = f32[1,1,1,256,256]{4,3,2,1,0:T(8,128)S(1)} collective-permute-done((f32[1,1,1,256,256]{4,3,2,1,0:T(8,128)S(1)}, f32[1,1,1,256,256]{4,3,2,1,0:T(8,128)S(1)}, u32[]{:S(2)}, u32[]{:S(2)}) %collective-permute-start.3) | collective-permute-done | bytes 262176 | tf_op jit(solution)/shard_map/ppermute | solution.py:25
  83.5 0.1 pad_maximum_fusion.1
  83.5 1.3 collective-permute-start.6
  84.8 3.1 %collective-permute-start.5 = (f32[1,3,1,256,256]{4,3,2,1,0:T(8,128)S(1)}, f32[1,3,1,256,256]{4,3,2,1,0:T(8,128)S(1)}, u32[]{:S(2)}, u32[]{:S(2)}) collective-permute-start(f32[1,3,1,256,256]{4,3,2,1,0:T(8,128)S(1)} %pad_maximum_fusion.1), channel_id=1, source_target_pairs={{0,8},{8,16},{16,24},{1,9},{9,17},{17,25},{2,10},{10,18},{18,26},{... | collective-permute-start | bytes 2359304 | tf_op jit(solution)/shard_map/ppermute | solution.py:25
  88.0 0.6 select_reduce_fusion.1.from_ref
  88.6 0.6 fusion.31.slot_ref
  89.1 0.6 bitcast_divide_fusion.share_ref
  89.7 0.0 collective-permute-done.5
  89.7 1.6 pad_maximum_fusion
  91.3 0.0 all-to-all-done
  91.4 14.8 %columns.1 = s16[4,8,400,128]{3,2,1,0:T(8,128)(2,1)} custom-call(s32[8]{0:T(128)} %select_reduce_fusion.1.from_ref, s32[4,64]{1,0:T(4,128)} %fusion.31.slot_ref, f32[4,64]{1,0:T(4,128)} %bitcast_divide_fusion.share_ref, bf16[256,64,96]{2,1,0:T(8,128)(2,1)} %bitcast.5.states_ref, f32[9,256,256]{2,1,0:T(8,128)} %bitcast.110), custom_call_target="tpu_custom_call" | custom-call | flops 1610612736 | bytes 6291456 | tf_op jit(solution)/shard_map/columns/pallas_call | solution.py:135
  106.1 15.0 %all-to-all-start.1 = ((s16[32,400,128]{2,1,0:T(8,128)(2,1)}), s16[32,400,128]{2,1,0:T(8,128)(2,1)S(1)}, u32[]{:S(2)}, u32[]{:S(2)}) async-start(s16[32,400,128]{2,1,0:T(8,128)(2,1)} %bitcast.109), calls=%async_computation.1 | async-start | bytes 6553600 | tf_op jit(solution)/shard_map/all_to_all | solution.py:260
  121.1 0.1 iota_add_fusion
  121.2 0.7 select_reduce_fusion.source_ref
  121.9 75.0 %all-to-all-done.1.code_ref = s16[32,400,128]{2,1,0:T(8,128)(2,1)S(1)} async-done(((s16[32,400,128]{2,1,0:T(8,128)(2,1)}), s16[32,400,128]{2,1,0:T(8,128)(2,1)S(1)}, u32[]{:S(2)}, u32[]{:S(2)}) %all-to-all-start.1) | async-done | bytes 3276832 | tf_op jit(solution)/shard_map/all_to_all | solution.py:260
  196.8 0.7 slice.4.tail_ref
  197.5 1.0 copy-done
  198.5 16.1 %native.1 = f32[2,48,64,256]{3,2,1,0:T(8,128)} custom-call(s32[32]{0:T(128)} %select_reduce_fusion.source_ref, s16[32,400,128]{2,1,0:T(8,128)(2,1)} %copy-done, s16[32,16,128]{2,1,0:T(8,128)(2,1)} %slice.4.tail_ref), custom_call_target="tpu_custom_call" | custom-call | tf_op jit(solution)/shard_map/native/pallas_call | solution.py:188
  (25 shorter events, 0.2 us)
Async XLA Ops:
  1.1 8.5 %collective-permute-start = (bf16[1,64,1024]{2,1,0:T(8,128)(2,1)S(1)}, bf16[1,64,1024]{2,1,0:T(8,128)(2,1)S(1)}, u32[]{:S(2)}, u32[]{:S(2)}) collective-permute-start(bf16[1,64,1024]{2,1,0:T(8,128)(2,1)S(1)} %get-tuple-element.9), channel_id=1, source_target_pairs={{0,24},{8,0},{16,8},{24,16},{1,25},{9,1},{17,9},{25,17},{2,26},{10... | collective-permute-start | bytes 393224 | tf_op jit(solution)/shard_map/ppermute | solution.py:40
  3.5 6.1 %collective-permute-start.1 = (bf16[1,64,1024]{2,1,0:T(8,128)(2,1)S(1)}, bf16[1,64,1024]{2,1,0:T(8,128)(2,1)S(1)}, u32[]{:S(2)}, u32[]{:S(2)}) collective-permute-start(bf16[1,64,1024]{2,1,0:T(8,128)(2,1)S(1)} %get-tuple-element.8), channel_id=1, source_target_pairs={{0,16},{8,24},{16,0},{24,8},{1,17},{9,25},{17,1},{25,9},{2,18},{10... | collective-permute-start | bytes 393224 | tf_op jit(solution)/shard_map/ppermute | solution.py:40
  4.2 54.5 %copy-start.1 = (bf16[4,1,1,64,1024]{4,3,2,1,0:T(8,128)(2,1)S(1)}, bf16[4,1,1,64,1024]{4,3,2,1,0:T(8,128)(2,1)}, u32[]{:S(2)}) copy-start(bf16[4,1,1,64,1024]{4,3,2,1,0:T(8,128)(2,1)} %param.8) | copy-start | bytes 1572868
  4.2 87.2 %all-to-all-start = ((bf16[4,64,64,96]{3,2,1,0:T(8,128)(2,1)}), bf16[4,64,64,96]{3,2,1,0:T(8,128)(2,1)}, u32[]{:S(2)}, u32[]{:S(2)}) async-start(bf16[4,64,64,96]{3,2,1,0:T(8,128)(2,1)} %bitcast.111), calls=%async_computation | async-start | bytes 8388608 | tf_op jit(solution)/shard_map/all_to_all | solution.py:211
  9.1 49.7 %copy-start.5 = (f32[1,1,1,1024]{3,2,1,0:T(1,128)S(1)}, f32[1,1,1,1024]{3,2,1,0:T(1,128)}, u32[]{:S(2)}) copy-start(f32[1,1,1,1024]{3,2,1,0:T(1,128)} %param.10) | copy-start | bytes 12292
  9.1 49.5 %collective-permute-start.2 = (bf16[1,64,1024]{2,1,0:T(8,128)(2,1)S(1)}, bf16[1,64,1024]{2,1,0:T(8,128)(2,1)S(1)}, u32[]{:S(2)}, u32[]{:S(2)}) collective-permute-start(bf16[1,64,1024]{2,1,0:T(8,128)(2,1)S(1)} %get-tuple-element.7), channel_id=1, source_target_pairs={{0,8},{8,16},{16,24},{24,0},{1,9},{9,17},{17,25},{25,1},{2,10},{10... | collective-permute-start | bytes 393224 | tf_op jit(solution)/shard_map/ppermute | solution.py:40
  66.1 1.7 copy-start.6
  66.9 8.7 %copy-start.3 = (f32[1,1,4,64]{3,2,1,0:T(4,128)S(1)}, f32[1,1,4,64]{3,2,1,0:T(4,128)}, u32[]{:S(2)}) copy-start(f32[1,1,4,64]{3,2,1,0:T(4,128)} %param.12) | copy-start | bytes 3076
  67.5 20.4 %copy-start.2 = (s32[4,8,8]{2,1,0:T(8,128)S(1)}, s32[4,8,8]{2,1,0:T(8,128)}, u32[]{:S(2)}) copy-start(s32[4,8,8]{2,1,0:T(8,128)} %param.13) | copy-start | bytes 3076
  67.5 21.1 %copy-start.4 = (s32[1,1,4,64]{3,2,1,0:T(4,128)S(1)}, s32[1,1,4,64]{3,2,1,0:T(4,128)}, u32[]{:S(2)}) copy-start(s32[1,1,4,64]{3,2,1,0:T(4,128)} %param.11) | copy-start | bytes 3076
  69.8 8.3 %collective-permute-start.4 = (f32[1,1,1,256,256]{4,3,2,1,0:T(8,128)S(1)}, f32[1,1,1,256,256]{4,3,2,1,0:T(8,128)S(1)}, u32[]{:S(2)}, u32[]{:S(2)}) collective-permute-start(f32[1,1,1,256,256]{4,3,2,1,0:T(8,128)S(1)} %add_bitcast_fusion), channel_id=1, source_target_pairs={{1,0},{2,1},{3,2},{4,3},{5,4},{6,5},{7,6},{9,8},{10,9},{11,10},{12... | collective-permute-start | bytes 786440 | tf_op jit(solution)/shard_map/ppermute | solution.py:28
  71.1 12.4 %collective-permute-start.3 = (f32[1,1,1,256,256]{4,3,2,1,0:T(8,128)S(1)}, f32[1,1,1,256,256]{4,3,2,1,0:T(8,128)S(1)}, u32[]{:S(2)}, u32[]{:S(2)}) collective-permute-start(f32[1,1,1,256,256]{4,3,2,1,0:T(8,128)S(1)} %add_bitcast_fusion), channel_id=1, source_target_pairs={{0,1},{1,2},{2,3},{3,4},{4,5},{5,6},{6,7},{8,9},{9,10},{10,11},{11... | collective-permute-start | bytes 786440 | tf_op jit(solution)/shard_map/ppermute | solution.py:25
  83.5 6.2 %collective-permute-start.6 = (f32[1,3,1,256,256]{4,3,2,1,0:T(8,128)S(1)}, f32[1,3,1,256,256]{4,3,2,1,0:T(8,128)S(1)}, u32[]{:S(2)}, u32[]{:S(2)}) collective-permute-start(f32[1,3,1,256,256]{4,3,2,1,0:T(8,128)S(1)} %pad_maximum_fusion.1), channel_id=1, source_target_pairs={{8,0},{16,8},{24,16},{9,1},{17,9},{25,17},{10,2},{18,10},{26,18},{... | collective-permute-start | bytes 2359304 | tf_op jit(solution)/shard_map/ppermute | solution.py:28
  84.8 4.9 %collective-permute-start.5 = (f32[1,3,1,256,256]{4,3,2,1,0:T(8,128)S(1)}, f32[1,3,1,256,256]{4,3,2,1,0:T(8,128)S(1)}, u32[]{:S(2)}, u32[]{:S(2)}) collective-permute-start(f32[1,3,1,256,256]{4,3,2,1,0:T(8,128)S(1)} %pad_maximum_fusion.1), channel_id=1, source_target_pairs={{0,8},{8,16},{16,24},{1,9},{9,17},{17,25},{2,10},{10,18},{18,26},{... | collective-permute-start | bytes 2359304 | tf_op jit(solution)/shard_map/ppermute | solution.py:25
  106.1 90.7 %all-to-all-start.1 = ((s16[32,400,128]{2,1,0:T(8,128)(2,1)}), s16[32,400,128]{2,1,0:T(8,128)(2,1)S(1)}, u32[]{:S(2)}, u32[]{:S(2)}) async-start(s16[32,400,128]{2,1,0:T(8,128)(2,1)} %bitcast.109), calls=%async_computation.1 | async-start | bytes 6553600 | tf_op jit(solution)/shard_map/all_to_all | solution.py:260
  196.8 1.7 copy-start
where the time goes:
time: 215 us
  waiting for transfers between devices  132 us (61%)
  starting transfers between devices  33.7 us (16%)
  Pallas kernels  30.8 us (14%)
  matrix products  9.55 us (4%)
  other arithmetic  4.59 us (2%)
  local copies, waits for them, and re-layouts  2.9 us (1%)
    all_to_all x1, waiting for transfers between devices, analysis_shards(): lax.all_to_all(outgoing, ('member', 'region'), split_axis=0, concat_axis=...  75 us
    ppermute x3, waiting for transfers between devices, band_members(): arrived.append(lax.ppermute(piece, axis, ring))  49 us
    pallas_call x1, Pallas kernels, blocks_to_native(): pl.pallas_call(functools.partial(native_kernel, places=places, block_size...  16.1 us
    all_to_all x1, starting transfers between devices, analysis_shards(): lax.all_to_all(outgoing, ('member', 'region'), split_axis=0, concat_axis=...  15 us
    pallas_call x1, Pallas kernels, columns_to_blocks(): pl.pallas_call(kernel, grid_spec=pltpu.PrefetchScalarGridSpec(num_scalar_...  14.8 us
    ppermute x2, starting transfers between devices, with_halo(): lax.ppermute(lax.slice_in_dim(block, block.shape[dim] - width, None, axis...  7.64 us
    ppermute x2, waiting for transfers between devices, with_halo(): lax.ppermute(lax.slice_in_dim(block, block.shape[dim] - width, None, axis...  5.43 us
    all_to_all x1, starting transfers between devices, analysis_shards(): lax.all_to_all(background[:, 0].transpose(0, 2, 3, 1), 'member', split_ax...  4.97 us
  transfers between devices with their start and end apart: 9, of which 4 were waited for; matrix products, arithmetic and copies ran while one was open for 7% of the time, Pallas kernels for 0%

commit v1 on v0

v1 whole, which is shorter than its diff:
```python
import functools
import math

import jax
import jax.numpy as jnp
from jax import lax
from jax.experimental import pallas as pl
from jax.experimental.pallas import tpu as pltpu
from jax.sharding import PartitionSpec as P

SWEEPS = 8
LANES = 128
CODE_TOP = 32700.0
LOG2E = 1.4426950408889634


def halo_pair(block, axis):
    count = lax.axis_size(axis)
    forward = [(i, i + 1) for i in range(count - 1)]
    backward = [(target, source) for source, target in forward]
    return lax.ppermute(block, axis, forward), lax.ppermute(block, axis, backward)


def band_members(pieces, axis):
    count = lax.axis_size(axis)
    here = lax.axis_index(axis)
    arrived = []
    for step in range(count - 1, 0, -1):
        piece = lax.dynamic_index_in_dim(pieces, (here + step) % count, 0, keepdims=False)
        ring = [(i, (i + step) % count) for i in range(count)]
        arrived.append(lax.ppermute(piece, axis, ring))
    return arrived


def halves(value):
    high = value.astype(jnp.bfloat16)
    return high, (value - high.astype(jnp.float32)).astype(jnp.bfloat16)


def product(left, right, contract=((1,), (0,))):
    def one(a, b):
        return lax.dot_general(a, b, (contract, ((), ())), preferred_element_type=jnp.float32)

    return one(left[0], right[0]) + (one(left[0], right[1]) + one(left[1], right[0]))


def transform_kernel(here_ref, value_ref, weight_ref, own_ref, *refs, member_count, fill):
    arrived, code_ref, group_ref = refs[:-2], refs[-2], refs[-1]
    width = own_ref.shape[2]
    members = member_count * width
    here = here_ref[0]
    group_ref[pl.ds(pl.multiple_of(here * width, width), width), :] = own_ref[0, 0].astype(
        jnp.float32
    )
    for i, piece in enumerate(arrived):
        source = (here + 1 + i) % member_count
        group_ref[pl.ds(pl.multiple_of(source * width, width), width), :] = piece[0].astype(
            jnp.float32
        )
    group = group_ref[...]
    mean = jnp.sum(group, axis=0, keepdims=True) * (1.0 / members)
    pert = group - mean
    departure = value_ref[0] - mean
    scaled = pert * weight_ref[0]
    gram = product(halves(scaled), halves(pert), ((1,), (1,)))
    forcing = jnp.sum(scaled * departure, axis=1, keepdims=True)
    rows_at = lax.broadcasted_iota(jnp.int32, (members, members), 0)
    columns_at = lax.broadcasted_iota(jnp.int32, (members, members), 1)
    identity = (rows_at == columns_at).astype(jnp.float32)
    system = gram + (members - 1.0) * identity
    norm = jnp.sqrt(
        jnp.sum(jnp.sum(system * system, axis=1, keepdims=True), axis=0, keepdims=True)
    )
    iterate = system / norm
    factor = 1.5 * identity - 0.5 * iterate
    inverse = factor
    iterate = product(halves(iterate), halves(factor))
    for sweep in range(1, SWEEPS):
        inverse_halves = halves(inverse)
        iterate_halves = halves(iterate)
        factor = 1.5 * identity - 0.5 * product(inverse_halves, iterate_halves)
        factor_halves = halves(factor)
        if sweep < SWEEPS - 1:
            iterate = product(iterate_halves, factor_halves)
        inverse = product(factor_halves, inverse_halves)
    first = jnp.sum(inverse * forcing, axis=0, keepdims=True)
    mean_weight = jnp.sum(inverse * first, axis=1, keepdims=True) / norm
    transform = jnp.sqrt((members - 1.0) / norm) * inverse + mean_weight
    total = jnp.sum(transform, axis=0, keepdims=True)
    transform = transform + (1.0 - total) * (1.0 / members)
    inner = width // fill
    transform = jnp.concatenate(
        [
            transform[(m * fill + q) * inner :][:inner]
            for q in range(fill)
            for m in range(member_count)
        ],
        axis=0,
    )
    values = transform.reshape(members // 8, 8, members)
    exponent = code_exponent(values)
    code = jnp.round(values * (1.0 / code_scale(exponent))[None])
    code_ref[0, :members, :] = code.astype(jnp.int32).reshape(members, members).astype(jnp.int16)
    tail = jnp.concatenate([exponent, exponent], axis=0).astype(jnp.int32)
    code_ref[0, members:, :] = tail.astype(jnp.int16)


def coded_transforms(obs_ensemble, obs_value, obs_weight, fill):
    member_count, points, width, observations = obs_ensemble.shape
    members = member_count * width
    here = lax.axis_index("member").astype(jnp.int32).reshape(1)
    arrived = band_members(obs_ensemble, "member")
    line = pl.BlockSpec((1, 1, observations), lambda n, h: (n, 0, 0))
    return pl.pallas_call(
        functools.partial(transform_kernel, member_count=member_count, fill=fill),
        grid_spec=pltpu.PrefetchScalarGridSpec(
            num_scalar_prefetch=1,
            grid=(points,),
            in_specs=[
                line,
                line,
                pl.BlockSpec((1, 1, width, observations), lambda n, h: (h[0], n, 0, 0)),
            ]
            + [pl.BlockSpec((1, width, observations), lambda n, h: (n, 0, 0))] * len(arrived),
            out_specs=pl.BlockSpec((1, members + 16, members), lambda n, h: (n, 0, 0)),
            scratch_shapes=[pltpu.VMEM((members, observations), jnp.float32)],
        ),
        out_shape=jax.ShapeDtypeStruct((points, members + 16, members), jnp.int16),
        name="transforms",
    )(here, obs_value[:, None], obs_weight[:, None], obs_ensemble, *arrived)


def code_exponent(values):
    top = jnp.max(jnp.abs(values), axis=0)
    return jnp.clip(jnp.ceil(jnp.log(top) * LOG2E), -100.0, 100.0)


def code_scale(exponent):
    return jnp.exp2(exponent) * (1.0 / CODE_TOP)


def pack_kernel(order_ref, states_ref, first_ref, second_ref, *, group):
    _, width, columns, levels = states_ref.shape
    fill = LANES // group
    inner = width // fill
    cut = first_ref.shape[1]
    lane_group = lax.broadcasted_iota(jnp.int32, (columns, LANES), 1) // group
    spare = jnp.zeros((columns, -levels % LANES), jnp.float32)
    for r in range(inner):
        source = [
            jnp.concatenate([states_ref[0, q * inner + r].astype(jnp.float32), spare], axis=1)
            for q in range(fill)
        ]
        for g in range(levels // group):
            tile, offset = divmod(g * group, LANES)
            joined = None
            for q in range(fill):
                piece = source[q][:, tile * LANES : (tile + 1) * LANES]
                shift = (q * group - offset) % LANES
                if shift:
                    piece = pltpu.roll(piece, shift, 1)
                joined = piece if joined is None else jnp.where(lane_group == q, piece, joined)
            if g < cut:
                first_ref[0, g, r] = joined.astype(jnp.bfloat16)
            else:
                second_ref[0, g - cut, r] = joined.astype(jnp.bfloat16)


def pack_lanes(states, order, cut):
    bands, width, columns, levels = states.shape
    group = math.gcd(levels, LANES)
    inner = width * group // LANES
    shapes = [(count, inner, columns, LANES) for count in (cut, levels // group - cut)]
    return pl.pallas_call(
        functools.partial(pack_kernel, group=group),
        grid_spec=pltpu.PrefetchScalarGridSpec(
            num_scalar_prefetch=1,
            grid=(bands,),
            in_specs=[pl.BlockSpec((1, width, columns, levels), lambda b, o: (o[b], 0, 0, 0))],
            out_specs=[
                pl.BlockSpec((1, *shapes[0]), lambda b, o: (o[b], 0, 0, 0, 0)),
                pl.BlockSpec((1, *shapes[1]), lambda b, o: (b, 0, 0, 0, 0)),
            ],
        ),
        out_shape=[jax.ShapeDtypeStruct((bands, *shape), jnp.bfloat16) for shape in shapes],
        name="pack",
    )(order, states)


def column_kernel(
    from_ref, slot_ref, share_ref, source_ref, *refs, member_count, block_size, levels, members,
    group,
):
    states_refs = refs[:-8]
    low_ref, own_ref, high_ref, out_ref, table_ref, rows_ref, mix_ref, wide_ref = refs[-8:]
    owner = pl.program_id(0)

    @pl.when(owner == 0)
    def _():
        for side, side_ref in enumerate((low_ref, own_ref, high_ref)):
            tiles = side_ref.shape[0]
            for n in range(tiles):
                tail = side_ref[n, members:, :].astype(jnp.int32).astype(jnp.float32)
                scale = code_scale(tail[:8])[None]

                def decode(r, carry):
                    start = pl.multiple_of(r * 64, 64)
                    code = side_ref[n, pl.ds(start, 64), :].astype(jnp.int32).astype(jnp.float32)
                    value = code.reshape(8, 8, members) * scale
                    table_ref[side * tiles + n, pl.ds(start, 64), :] = value.reshape(64, members)
                    return carry

                lax.fori_loop(0, members // 64, decode, 0)

    first_column = from_ref[owner] * block_size
    width = members // member_count
    folds = max(1, LANES // width)
    rows = levels // folds
    fill = LANES // group
    groups = levels // group
    inner = width // fill
    packed = member_count * groups * inner
    for n, states_ref in enumerate(states_refs):
        height = states_ref.shape[0] * block_size
        start = pl.multiple_of(source_ref[n] * height, height)
        rows_ref[pl.ds(start, height), :] = (
            states_ref[...].astype(jnp.float32).reshape(height, LANES)
        )
    lane_group = lax.broadcasted_iota(jnp.int32, (rows, LANES), 1) // width
    strip = 32
    for i in range(block_size):
        column = first_column + i
        slots = [slot_ref[s, column] for s in range(4)]
        shares = [share_ref[s, column] for s in range(4)]
        buffer = i % 2
        for r in range(0, members, strip):
            mixed = shares[0] * table_ref[slots[0], r : r + strip, :]
            for s in range(1, 4):
                mixed = mixed + shares[s] * table_ref[slots[s], r : r + strip, :]
            high = mixed.astype(jnp.bfloat16)
            low = (mixed - high.astype(jnp.float32)).astype(jnp.bfloat16)
            mix_ref[buffer, r : r + strip, :] = high
            mix_ref[buffer, members + r : members + r + strip, :] = low
        dense = rows_ref[pl.ds(i, packed, stride=block_size), :]
        lines = []
        for g in range(groups):
            part = jnp.concatenate(
                [dense[(m * groups + g) * inner :][:inner] for m in range(member_count)], axis=0
            )
            turned = part.astype(jnp.bfloat16).T
            lines.append(
                jnp.concatenate([turned[q * group : (q + 1) * group] for q in range(fill)], axis=1)
            )
        state = jnp.concatenate(lines, axis=0)
        fresh = jnp.dot(
            jnp.concatenate([state, state], axis=1), mix_ref[buffer],
            preferred_element_type=jnp.float32,
        )
        for m in range(member_count):
            tile, offset = divmod(m * width, LANES)
            joined = None
            for h in range(folds):
                piece = jnp.concatenate(
                    [fresh[(t * folds + h) * 8 :][:8] for t in range(rows // 8)], axis=0
                )[:, tile * LANES : (tile + 1) * LANES]
                shift = (h * width - offset) % LANES
                if shift:
                    piece = pltpu.roll(piece, shift, 1)
                joined = piece if joined is None else jnp.where(lane_group == h, piece, joined)
            wide_ref[m, pl.ds(i, rows, stride=block_size), :] = joined
    for m in range(member_count):
        values = wide_ref[m].reshape(rows, block_size, LANES)
        exponent = code_exponent(values)
        code = jnp.round(values * (1.0 / code_scale(exponent))[None])
        code = code.astype(jnp.int32).reshape(rows * block_size, LANES)
        out_ref[m, 0, : rows * block_size, :] = code.astype(jnp.int16)
        out_ref[m, 0, rows * block_size :, :] = exponent.astype(jnp.int32).astype(jnp.int16)


def columns_to_blocks(
    states, source, sides, slots, share, send_from, group, levels, member_count, block_size
):
    tiles, _, members = sides[0].shape
    columns = states[0].shape[1]
    patches = send_from.shape[0]
    packed = sum(piece.shape[0] for piece in states)
    width = members // member_count
    folds = max(1, LANES // width)
    rows = levels // folds
    coded = (rows + 1) * block_size
    kernel = functools.partial(
        column_kernel, member_count=member_count, block_size=block_size, levels=levels,
        members=members, group=group,
    )
    return pl.pallas_call(
        kernel,
        grid_spec=pltpu.PrefetchScalarGridSpec(
            num_scalar_prefetch=4,
            grid=(patches,),
            in_specs=[
                pl.BlockSpec((piece.shape[0], block_size, LANES), lambda o, f, a, b, c: (0, f[o], 0))
                for piece in states
            ]
            + [pl.BlockSpec(sides[0].shape, lambda o, f, a, b, c: (0, 0, 0))] * len(sides),
            out_specs=pl.BlockSpec(
                (member_count, 1, coded, LANES), lambda o, f, a, b, c: (0, o, 0, 0)
            ),
            scratch_shapes=[
                pltpu.VMEM((len(sides) * tiles, members, members), jnp.float32),
                pltpu.VMEM((packed * block_size, LANES), jnp.float32),
                pltpu.VMEM((2, 2 * members, members), jnp.bfloat16),
                pltpu.VMEM((member_count, rows * block_size, LANES), jnp.float32),
            ],
        ),
        out_shape=jax.ShapeDtypeStruct((member_count, patches, coded, LANES), jnp.int16),
        cost_estimate=pl.CostEstimate(
            flops=4 * columns * levels * members * members, transcendentals=0,
            bytes_accessed=4 * packed * columns * LANES,
        ),
        name="columns",
    )(send_from, slots, share, source, *states, *sides)


def native_kernel(source_ref, code_ref, *refs, places, block_size, tail_at):
    out_ref, scale_ref = refs[-2:]
    height, width, _ = out_ref.shape
    folds = max(1, LANES // width)
    strip = height // folds
    pair = 2 * block_size

    @pl.when(pl.program_id(0) == 0)
    def _():
        for t in range(places):
            tail = code_ref[source_ref[t], tail_at : tail_at + block_size, :]
            scale_ref[t] = code_scale(tail.astype(jnp.int32).astype(jnp.float32))

    first = pl.program_id(0) * (strip * block_size)
    for r in range(0, strip, 2):
        start = pl.multiple_of(first + r * block_size, pair)
        pieces = [
            code_ref[source_ref[t], pl.ds(start, pair), :].astype(jnp.int32).astype(jnp.float32)
            for t in range(places)
        ]
        for half in range(2):
            stacked = jnp.concatenate(
                [
                    piece[half * block_size : (half + 1) * block_size] * scale_ref[t]
                    for t, piece in enumerate(pieces)
                ],
                axis=0,
            )
            turned = stacked.T
            for h in range(folds):
                out_ref[h * strip + r + half] = turned[h * width : (h + 1) * width]


def blocks_to_native(incoming, arrive_from, previous, width, levels, from_level, block_size):
    _, coded, _ = incoming.shape
    places = arrive_from.shape[0]
    folds = max(1, LANES // width)
    tail_at = coded - block_size
    height = 8 * folds
    first = from_level // height
    return pl.pallas_call(
        functools.partial(native_kernel, places=places, block_size=block_size, tail_at=tail_at),
        grid_spec=pltpu.PrefetchScalarGridSpec(
            num_scalar_prefetch=1,
            grid=(tail_at // block_size // 8,),
            in_specs=[pl.BlockSpec(memory_space=pltpu.VMEM)]
            + [pl.BlockSpec(memory_space=pl.ANY)] * len(previous),
            out_specs=pl.BlockSpec(
                (height, width, places * block_size), lambda g, a: (first + g, 0, 0)
            ),
            scratch_shapes=[pltpu.VMEM((places, block_size, LANES), jnp.float32)],
        ),
        out_shape=jax.ShapeDtypeStruct((levels, width, places * block_size), jnp.float32),
        input_output_aliases={2: 0} if previous else {},
        name="native",
    )(arrive_from, incoming, *previous)


def analysis_shards(
    background, obs_ensemble, obs_value, obs_weight, stencil, stencil_weight, block_target
):
    members = obs_ensemble.shape[3] * lax.axis_size("member")
    fill = LANES // math.gcd(background.shape[2], LANES)
    coded = coded_transforms(obs_ensemble[:, 0], obs_value[0, 0], obs_weight[0, 0], fill)
    points = coded.shape[0]
    member_count = lax.axis_size("member")
    band_index = lax.axis_index("member")
    levels, columns = background.shape[2], background.shape[4]
    group = math.gcd(levels, LANES)
    groups = levels // group
    cut = max(1, groups // 3)
    order = (band_index + jnp.arange(member_count, dtype=jnp.int32)) % member_count
    early, late = pack_lanes(background[:, 0].transpose(0, 2, 3, 1), order, cut)
    early = lax.all_to_all(early, "member", split_axis=0, concat_axis=0, tiled=True)
    late = [late[step] for step in range(member_count)]
    left, right = halo_pair(coded, "region")
    left, *late = lax.optimization_barrier((left, *late))
    trio = jnp.concatenate([left, coded, right], axis=0)
    low, high = halo_pair(trio, "member")
    late_pieces = [late[0].reshape(-1, columns, LANES)]
    for step in range(1, member_count):
        ring = [(i, (i + step) % member_count) for i in range(member_count)]
        arrived = lax.ppermute(late[step], "member", ring)
        late_pieces.append(arrived.reshape(-1, columns, LANES))
    late_source = (band_index - jnp.arange(member_count, dtype=jnp.int32)) % member_count
    early_source = jnp.zeros((1,), jnp.int32)
    patch_index = lax.axis_index("region")
    patch_list = lax.axis_size("region")
    shard_width = members // member_count
    stencil_rows = stencil[0, 0]
    near_band = stencil_rows // (patch_list * points)
    near_patch = stencil_rows // points % patch_list
    local_index = (
        (near_band - band_index + 1) * 3 + (near_patch - patch_index + 1)
    ) * points + stencil_rows % points
    share = stencil_weight[0, 0] / jnp.sum(stencil_weight[0, 0], axis=0, keepdims=True)
    band_count = block_target.shape[0]
    per_device = block_target.shape[2]
    per_owner = band_count * per_device
    block_size = columns // per_device
    owners = block_target // per_owner
    places = block_target % per_owner
    patch_ids = jnp.arange(patch_list, dtype=jnp.int32)
    place_ids = jnp.arange(per_owner, dtype=jnp.int32)
    band_owners = lax.dynamic_index_in_dim(owners, band_index, 0, keepdims=False)
    my_owners = lax.dynamic_index_in_dim(band_owners, patch_index, 0, keepdims=False)
    block_ids = jnp.arange(per_device, dtype=jnp.int32)
    send_hit = my_owners[None, :] == patch_ids[:, None]
    send_from = jnp.sum(send_hit.astype(jnp.int32) * block_ids[None, :], axis=1)
    band_ids = jnp.arange(band_count, dtype=jnp.int32)
    source = band_ids[:, None, None] * patch_list + patch_ids[None, :, None] + 0 * places
    arrive_hit = (owners == patch_index)[None] & (places[None] == place_ids[:, None, None, None])
    arrive_from = jnp.sum(arrive_hit.astype(jnp.int32) * source[None], axis=(1, 2, 3))
    native = ()
    chunks = (
        (0, cut, [early.reshape(-1, columns, LANES)], early_source),
        (cut, groups, late_pieces, late_source),
    )
    for start, end, states, state_source in chunks:
        outgoing = columns_to_blocks(
            states, state_source, (low, trio, high), local_index, share, send_from, group,
            (end - start) * group, member_count, block_size,
        )
        outgoing = outgoing.reshape(member_count * patch_list, *outgoing.shape[2:])
        incoming = lax.all_to_all(
            outgoing, ("member", "region"), split_axis=0, concat_axis=0, tiled=True
        )
        native = (
            blocks_to_native(
                incoming, arrive_from, native, shard_width, levels, start * group, block_size
            ),
        )
    return native[0].reshape(1, levels, shard_width, per_owner * block_size)


def solution(mesh):
    in_specs = (
        P(None, "region", None, "member", None),
        P(None, "region", None, "member", None),
        P("member", "region", None, None),
        P("member", "region", None, None),
        P("member", "region", None, None),
        P("member", "region", None, None),
        P(),
    )
    out_specs = P("region", None, "member", None)
    return jax.shard_map(analysis_shards, mesh=mesh, in_specs=in_specs, out_specs=out_specs, check_vma=False)
```

time: 215 us -> 186 us (0.87)
  waiting for transfers between devices: 132 us -> 82.2 us
  Pallas kernels: 30.8 us -> 49.6 us
  matrix products: 9.55 us -> 0 us
  starting transfers between devices: 33.7 us -> 38.5 us
  local copies, waits for them, and re-layouts: 2.9 us -> 6.87 us
  other arithmetic: 4.59 us -> 7.32 us
    ppermute x3, waiting for transfers between devices: 49 us -> 0.01 us  [band_members(): arrived.append(lax.ppermute(piece, axis, ring))]
    all_to_all x1 -> x2, waiting for transfers between devices: 75 us -> 47 us  [analysis_shards(): lax.all_to_all(outgoing, ('member', 'region'), split_axis=0, concat_axis=...]
    ppermute x4 -> x7, waiting for transfers between devices: 7.79 us -> 35.2 us  [the longest x3 31.3 us: analysis_shards(): arrived = lax.ppermute(late[step], 'member', ring)]
    pallas_call x0 -> x2, Pallas kernels: none -> 14.5 us  [the longest x1 8.15 us: coded_transforms(): pl.pallas_call(functools.partial(transform_kernel, member_count=member_co...]
    pallas_call x1 -> x2, Pallas kernels: 14.8 us -> 26.1 us  [columns_to_blocks(): pl.pallas_call(kernel, grid_spec=pltpu.PrefetchScalarGridSpec(num_scalar_...]
    dot_general x27 -> x0, matrix products: 9.55 us -> none  [the longest x8 2.16 us: build_transforms(): jnp.matmul(inverse, iterate, precision=three_pass)]
    pallas_call x1 -> x2, Pallas kernels: 16.1 us -> 9.05 us  [blocks_to_native(): pl.pallas_call(functools.partial(native_kernel, places=places, block_size...]
    unnamed x21 -> x30, local copies, waits for them, and re-layouts: 1.12 us -> 4.44 us
  transfers between devices with their start and end apart: 9 -> 13, of which waited for: 4 -> 5; matrix products, arithmetic and copies ran while one was open for 7% -> 5% of each run, Pallas kernels for 0% -> 17%
where the time goes in v1:
time: 186 us; the launch traced here: 185 us
  waiting for transfers between devices  82.2 us (44%)
  Pallas kernels  49.6 us (27%)
  starting transfers between devices  38.5 us (21%)
  other arithmetic  7.32 us (4%)
  local copies, waits for them, and re-layouts  6.87 us (4%)
    all_to_all x2, waiting for transfers between devices, analysis_shards(): lax.all_to_all(outgoing, ('member', 'region'), split_axis=0, concat_axis=...  47 us
    ppermute x3, waiting for transfers between devices, analysis_shards(): arrived = lax.ppermute(late[step], 'member', ring)  31.3 us
    pallas_call x2, Pallas kernels, columns_to_blocks(): pl.pallas_call(kernel, grid_spec=pltpu.PrefetchScalarGridSpec(num_scalar_...  26.1 us
    all_to_all x2, starting transfers between devices, analysis_shards(): lax.all_to_all(outgoing, ('member', 'region'), split_axis=0, concat_axis=...  16.7 us
    pallas_call x2, Pallas kernels, blocks_to_native(): pl.pallas_call(functools.partial(native_kernel, places=places, block_size...  9.05 us
    pallas_call x1, Pallas kernels, coded_transforms(): pl.pallas_call(functools.partial(transform_kernel, member_count=member_co...  8.15 us
    ppermute x2, starting transfers between devices, halo_pair(): lax.ppermute(block, axis, forward)  7.61 us
    pallas_call x1, Pallas kernels, pack_lanes(): pl.pallas_call(functools.partial(pack_kernel, group=group), grid_spec=plt...  6.39 us
  transfers between devices with their start and end apart: 13, of which 5 were waited for; matrix products, arithmetic and copies ran while one was open for 5% of the time, Pallas kernels for 17%

profile of v1, /device:TPU:0, one launch (start us, length us, event | category | flops | bytes accessed | tf_op | source)
XLA Modules:
  0.0 184.8 jit_solution(16160234454161977019)
XLA Ops:
  0.0 1.1 dynamic-slice_bitcast_fusion
  1.1 0.5 collective-permute-start.2
  1.6 2.0 %collective-permute-start = (bf16[1,64,1024]{2,1,0:T(8,128)(2,1)S(1)}, bf16[1,64,1024]{2,1,0:T(8,128)(2,1)}, u32[]{:S(2)}, u32[]{:S(2)}) collective-permute-start(bf16[1,64,1024]{2,1,0:T(8,128)(2,1)S(1)} %get-tuple-element.26), channel_id=1, source_target_pairs={{0,24},{8,0},{16,8},{24,16},{1,25},{9,1},{17,9},{25,17},{2,26},{10... | collective-permute-start | bytes 393224 | tf_op jit(solution)/shard_map/ppermute | solution.py:31
  3.6 2.2 %collective-permute-start.1 = (bf16[1,64,1024]{2,1,0:T(8,128)(2,1)S(1)}, bf16[1,64,1024]{2,1,0:T(8,128)(2,1)}, u32[]{:S(2)}, u32[]{:S(2)}) collective-permute-start(bf16[1,64,1024]{2,1,0:T(8,128)(2,1)S(1)} %get-tuple-element.27), channel_id=1, source_target_pairs={{0,16},{8,24},{16,0},{24,8},{1,17},{9,25},{17,1},{25,9},{2,18},{10... | collective-permute-start | bytes 393224 | tf_op jit(solution)/shard_map/ppermute | solution.py:31
  5.8 0.6 and_select_fusion.order_ref
  6.4 6.4 %pack.1 = (bf16[4,1,16,64,128]{4,3,2,1,0:T(8,128)(2,1)}, bf16[4,2,16,64,128]{4,3,2,1,0:T(8,128)(2,1)}) custom-call(s32[4]{0:T(128)} %and_select_fusion.order_ref, bf16[4,64,64,96]{3,2,1,0:T(8,128)(2,1)} %bitcast.52), custom_call_target="tpu_custom_call" | custom-call | tf_op jit(solution)/shard_map/pack/pallas_call | solution.py:174
  12.8 3.6 %all-to-all-start.1 = ((bf16[4,1,16,64,128]{4,3,2,1,0:T(8,128)(2,1)}), bf16[4,1,16,64,128]{4,3,2,1,0:T(8,128)(2,1)S(1)}, u32[]{:S(2)}, u32[]{:S(2)}) async-start(bf16[4,1,16,64,128]{4,3,2,1,0:T(8,128)(2,1)} %get-tuple-element.18), calls=%async_computation.1 | async-start | bytes 2097152 | tf_op jit(solution)/shard_map/all_to_all | solution.py:397
  16.5 0.0 copy-start.13
  16.5 0.0 copy-done.4
  16.5 1.4 slice_bitcast_fusion
  17.9 0.0 copy-done.13
  17.9 0.6 broadcast_compare_fusion
  18.4 0.0 collective-permute-done.2.refs_2_
  18.4 0.0 collective-permute-done.refs_0_
  18.5 0.0 collective-permute-done.1.refs_1_
  18.5 8.2 %transforms.1 = s16[1,272,256]{2,1,0:T(8,128)(2,1)} custom-call(s32[1]{0:T(128)} %bitcast.3.here_ref, f32[1,1,1024]{2,1,0:T(1,128)} %bitcast.58, f32[1,1,1024]{2,1,0:T(1,128)} %bitcast.59, bf16[4,1,64,1024]{3,2,1,0:T(8,128)(2,1)} %bitcast.54, bf16[1,64,1024]{2,1,0:T(8,128)(2,1)} %collective-permute-done.refs_0_, ...), custom_call_target="tpu_custom_call" | custom-call | tf_op jit(solution)/shard_map/transforms/pallas_call | solution.py:114
  26.6 1.3 collective-permute-start.7
  27.9 4.6 %collective-permute-start.3 = (s16[1,272,256]{2,1,0:T(8,128)(2,1)}, s16[1,272,256]{2,1,0:T(8,128)(2,1)S(1)}, u32[]{:S(2)}, u32[]{:S(2)}) collective-permute-start(s16[1,272,256]{2,1,0:T(8,128)(2,1)} %transforms.1), channel_id=1, source_target_pairs={{0,1},{1,2},{2,3},{3,4},{4,5},{5,6},{6,7},{8,9},{9,10},{10,11},{11... | collective-permute-start | bytes 417800 | tf_op jit(solution)/shard_map/ppermute | solution.py:21
  32.5 0.7 reduce_sum.29
  33.2 0.6 select_reduce_fusion.1.from_ref
  33.8 3.9 %collective-permute-done.3 = s16[1,272,256]{2,1,0:T(8,128)(2,1)S(1)} collective-permute-done((s16[1,272,256]{2,1,0:T(8,128)(2,1)}, s16[1,272,256]{2,1,0:T(8,128)(2,1)S(1)}, u32[]{:S(2)}, u32[]{:S(2)}) %collective-permute-start.3) | collective-permute-done | bytes 139296 | tf_op jit(solution)/shard_map/ppermute | solution.py:21
  37.7 0.0 collective-permute-done.7
  37.8 0.9 pad_add_fusion.refs_5_.refs_2_
  38.7 0.0 copy-start.3
  38.7 1.3 collective-permute-start.9
  40.0 3.1 %collective-permute-start.8 = (s16[3,272,256]{2,1,0:T(8,128)(2,1)S(1)}, s16[3,272,256]{2,1,0:T(8,128)(2,1)S(1)}, u32[]{:S(2)}, u32[]{:S(2)}) collective-permute-start(s16[3,272,256]{2,1,0:T(8,128)(2,1)S(1)} %pad_add_fusion.refs_5_.refs_2_), channel_id=1, source_target_pairs={{0,8},{8,16},{16,24},{1,9},{9,17},{17,25},{2,10},{10,18},{18,26},{... | collective-permute-start | bytes 1253384 | tf_op jit(solution)/shard_map/ppermute | solution.py:21
  43.1 1.3 fusion.6.slot_ref
  44.3 1.3 bitcast_divide_fusion.share_ref
  45.6 0.0 collective-permute-done.9.refs_6_.refs_3_
  45.6 0.0 collective-permute-done.8.refs_4_.refs_1_
  45.6 0.0 copy-start.6
  45.6 0.0 all-to-all-done.1
  45.6 0.0 copy-start.2
  45.7 0.0 copy-done.3
  45.7 0.8 copy-done.5
  46.4 0.1 copy-done.6
  46.6 0.3 copy-done.2
  46.9 12.3 %columns.3 = s16[4,8,136,128]{3,2,1,0:T(8,128)(2,1)} custom-call(s32[8]{0:T(128)} %select_reduce_fusion.1.from_ref, s32[4,64]{1,0:T(4,128)} %fusion.6.slot_ref, f32[4,64]{1,0:T(4,128)} %bitcast_divide_fusion.share_ref, s32[1]{0:T(128)} %constant.157.clone.1.source_ref, bf16[64,64,128]{2,1,0:T(8,128)(2,1)} %bitcast.51, s16[3,272,256]{2,1,0:T(8,128)(2,1)} %copy-done.6, ...), custom_call_target="tpu_custom_call" | custom-call | flops 536870912 | bytes 2097152 | tf_op jit(solution)/shard_map/columns/pallas_call | solution.py:295
  59.2 10.2 %all-to-all-start.2 = ((s16[32,136,128]{2,1,0:T(8,128)(2,1)}), s16[32,136,128]{2,1,0:T(8,128)(2,1)S(1)}, u32[]{:S(2)}, u32[]{:S(2)}) async-start(s16[32,136,128]{2,1,0:T(8,128)(2,1)} %bitcast.50), calls=%async_computation.2 | async-start | bytes 2228224 | tf_op jit(solution)/shard_map/all_to_all | solution.py:448
  69.4 0.0 copy-done.9
  69.4 0.3 collective-permute-start.4
  69.7 0.0 copy-done.8
  69.7 1.6 collective-permute-start.5
  71.3 0.0 copy-done.7
  71.3 1.4 collective-permute-start.6
  72.7 0.5 and_select_fusion.1.source_ref
  73.2 20.1 %collective-permute-done.4 = bf16[2,16,64,128]{3,2,1,0:T(8,128)(2,1)S(1)} collective-permute-done((bf16[2,16,64,128]{3,2,1,0:T(8,128)(2,1)S(1)}, bf16[2,16,64,128]{3,2,1,0:T(8,128)(2,1)S(1)}, u32[]{:S(2)}, u32[]{:S(2)}) %collective-permute-start.4) | collective-permute-done | bytes 524320 | tf_op jit(solution)/shard_map/ppermute | solution.py:406
  93.3 1.3 collective-permute-done.5
  94.6 9.9 %collective-permute-done.6 = bf16[2,16,64,128]{3,2,1,0:T(8,128)(2,1)S(1)} collective-permute-done((bf16[2,16,64,128]{3,2,1,0:T(8,128)(2,1)S(1)}, bf16[2,16,64,128]{3,2,1,0:T(8,128)(2,1)S(1)}, u32[]{:S(2)}, u32[]{:S(2)}) %collective-permute-start.6) | collective-permute-done | bytes 524320 | tf_op jit(solution)/shard_map/ppermute | solution.py:406
  104.5 0.0 copy-done.11
  104.5 0.8 copy-done.12
  105.3 0.0 copy-done.10
  105.3 13.8 %columns.2 = s16[4,8,264,128]{3,2,1,0:T(8,128)(2,1)} custom-call(s32[8]{0:T(128)} %select_reduce_fusion.1.from_ref, s32[4,64]{1,0:T(4,128)} %fusion.6.slot_ref, f32[4,64]{1,0:T(4,128)} %bitcast_divide_fusion.share_ref, s32[4]{0:T(128)} %and_select_fusion.1.source_ref, bf16[32,64,128]{2,1,0:T(8,128)(2,1)} %bitcast.53, bf16[32,64,128]{2,1,0:T(8,128)(2,1)} %bitcast.55, ...), custom_call_target="tpu_custom_call" | custom-call | flops 1073741824 | bytes 4194304 | tf_op jit(solution)/shard_map/columns/pallas_call | solution.py:295
  119.1 0.0 all-to-all-done.2.code_ref
  119.1 0.0 copy-start.14
  119.1 1.0 copy-done.1
  120.1 6.5 %all-to-all-start = ((s16[32,264,128]{2,1,0:T(8,128)(2,1)}), s16[32,264,128]{2,1,0:T(8,128)(2,1)S(1)}, u32[]{:S(2)}, u32[]{:S(2)}) async-start(s16[32,264,128]{2,1,0:T(8,128)(2,1)} %bitcast.49), calls=%async_computation | async-start | bytes 4325376 | tf_op jit(solution)/shard_map/all_to_all | solution.py:448
  126.6 0.1 iota_add_fusion
  126.7 0.0 copy-done.14
  126.7 0.7 select_reduce_fusion.source_ref
  127.4 3.7 %native.2.refs_0_ = f32[96,64,256]{2,1,0:T(8,128)} custom-call(s32[32]{0:T(128)} %select_reduce_fusion.source_ref, s16[32,136,128]{2,1,0:T(8,128)(2,1)} %copy-done.1), custom_call_target="tpu_custom_call" | custom-call | tf_op jit(solution)/shard_map/native/pallas_call | solution.py:364
  131.1 47.0 %all-to-all-done.code_ref = s16[32,264,128]{2,1,0:T(8,128)(2,1)S(1)} async-done(((s16[32,264,128]{2,1,0:T(8,128)(2,1)}), s16[32,264,128]{2,1,0:T(8,128)(2,1)S(1)}, u32[]{:S(2)}, u32[]{:S(2)}) %all-to-all-start) | async-done | bytes 2162720 | tf_op jit(solution)/shard_map/all_to_all | solution.py:448
  178.1 1.4 copy-done
  179.4 5.4 %native.3 = f32[96,64,256]{2,1,0:T(8,128)} custom-call(s32[32]{0:T(128)} %select_reduce_fusion.source_ref, s16[32,264,128]{2,1,0:T(8,128)(2,1)} %copy-done, f32[96,64,256]{2,1,0:T(8,128)} %native.2.refs_0_), custom_call_target="tpu_custom_call", output_to_operand_aliasing={{}: (2, {})} | custom-call | tf_op jit(solution)/shard_map/native/pallas_call | solution.py:364
  (13 shorter events, 0.0 us)
Async XLA Ops:
  1.1 17.4 %collective-permute-start.2 = (bf16[1,64,1024]{2,1,0:T(8,128)(2,1)S(1)}, bf16[1,64,1024]{2,1,0:T(8,128)(2,1)}, u32[]{:S(2)}, u32[]{:S(2)}) collective-permute-start(bf16[1,64,1024]{2,1,0:T(8,128)(2,1)S(1)} %get-tuple-element.25), channel_id=1, source_target_pairs={{0,8},{8,16},{16,24},{24,0},{1,9},{9,17},{17,25},{25,1},{2,10},{10... | collective-permute-start | bytes 393224 | tf_op jit(solution)/shard_map/ppermute | solution.py:31
  1.6 16.8 %collective-permute-start = (bf16[1,64,1024]{2,1,0:T(8,128)(2,1)S(1)}, bf16[1,64,1024]{2,1,0:T(8,128)(2,1)}, u32[]{:S(2)}, u32[]{:S(2)}) collective-permute-start(bf16[1,64,1024]{2,1,0:T(8,128)(2,1)S(1)} %get-tuple-element.26), channel_id=1, source_target_pairs={{0,24},{8,0},{16,8},{24,16},{1,25},{9,1},{17,9},{25,17},{2,26},{10... | collective-permute-start | bytes 393224 | tf_op jit(solution)/shard_map/ppermute | solution.py:31
  3.6 14.9 %collective-permute-start.1 = (bf16[1,64,1024]{2,1,0:T(8,128)(2,1)S(1)}, bf16[1,64,1024]{2,1,0:T(8,128)(2,1)}, u32[]{:S(2)}, u32[]{:S(2)}) collective-permute-start(bf16[1,64,1024]{2,1,0:T(8,128)(2,1)S(1)} %get-tuple-element.27), channel_id=1, source_target_pairs={{0,16},{8,24},{16,0},{24,8},{1,17},{9,25},{17,1},{25,9},{2,18},{10... | collective-permute-start | bytes 393224 | tf_op jit(solution)/shard_map/ppermute | solution.py:31
  12.8 3.7 %copy-start.4 = (bf16[4,2,16,64,128]{4,3,2,1,0:T(8,128)(2,1)S(1)}, bf16[4,2,16,64,128]{4,3,2,1,0:T(8,128)(2,1)}, u32[]{:S(2)}) copy-start(bf16[4,2,16,64,128]{4,3,2,1,0:T(8,128)(2,1)} %get-tuple-element.12) | copy-start | bytes 6291460
  12.8 32.8 %all-to-all-start.1 = ((bf16[4,1,16,64,128]{4,3,2,1,0:T(8,128)(2,1)}), bf16[4,1,16,64,128]{4,3,2,1,0:T(8,128)(2,1)S(1)}, u32[]{:S(2)}, u32[]{:S(2)}) async-start(bf16[4,1,16,64,128]{4,3,2,1,0:T(8,128)(2,1)} %get-tuple-element.18), calls=%async_computation.1 | async-start | bytes 2097152 | tf_op jit(solution)/shard_map/all_to_all | solution.py:397
  16.5 1.4 copy-start.13
  26.6 11.1 %collective-permute-start.7 = (s16[1,272,256]{2,1,0:T(8,128)(2,1)}, s16[1,272,256]{2,1,0:T(8,128)(2,1)S(1)}, u32[]{:S(2)}, u32[]{:S(2)}) collective-permute-start(s16[1,272,256]{2,1,0:T(8,128)(2,1)} %transforms.1), channel_id=1, source_target_pairs={{1,0},{2,1},{3,2},{4,3},{5,4},{6,5},{7,6},{9,8},{10,9},{11,10},{12... | collective-permute-start | bytes 417800 | tf_op jit(solution)/shard_map/ppermute | solution.py:21
  27.9 9.8 %collective-permute-start.3 = (s16[1,272,256]{2,1,0:T(8,128)(2,1)}, s16[1,272,256]{2,1,0:T(8,128)(2,1)S(1)}, u32[]{:S(2)}, u32[]{:S(2)}) collective-permute-start(s16[1,272,256]{2,1,0:T(8,128)(2,1)} %transforms.1), channel_id=1, source_target_pairs={{0,1},{1,2},{2,3},{3,4},{4,5},{5,6},{6,7},{8,9},{9,10},{10,11},{11... | collective-permute-start | bytes 417800 | tf_op jit(solution)/shard_map/ppermute | solution.py:21
  38.7 7.0 %copy-start.3 = (s16[3,272,256]{2,1,0:T(8,128)(2,1)}, s16[3,272,256]{2,1,0:T(8,128)(2,1)S(1)}, u32[]{:S(2)}) copy-start(s16[3,272,256]{2,1,0:T(8,128)(2,1)S(1)} %pad_add_fusion.refs_5_.refs_2_) | copy-start | bytes 1253380
  38.7 6.9 %collective-permute-start.9 = (s16[3,272,256]{2,1,0:T(8,128)(2,1)S(1)}, s16[3,272,256]{2,1,0:T(8,128)(2,1)S(1)}, u32[]{:S(2)}, u32[]{:S(2)}) collective-permute-start(s16[3,272,256]{2,1,0:T(8,128)(2,1)S(1)} %pad_add_fusion.refs_5_.refs_2_), channel_id=1, source_target_pairs={{8,0},{16,8},{24,16},{9,1},{17,9},{25,17},{10,2},{18,10},{26,18},{... | collective-permute-start | bytes 1253384 | tf_op jit(solution)/shard_map/ppermute | solution.py:21
  40.0 5.6 %collective-permute-start.8 = (s16[3,272,256]{2,1,0:T(8,128)(2,1)S(1)}, s16[3,272,256]{2,1,0:T(8,128)(2,1)S(1)}, u32[]{:S(2)}, u32[]{:S(2)}) collective-permute-start(s16[3,272,256]{2,1,0:T(8,128)(2,1)S(1)} %pad_add_fusion.refs_5_.refs_2_), channel_id=1, source_target_pairs={{0,8},{8,16},{16,24},{1,9},{9,17},{17,25},{2,10},{10,18},{18,26},{... | collective-permute-start | bytes 1253384 | tf_op jit(solution)/shard_map/ppermute | solution.py:21
  45.6 0.8 copy-start.5
  45.6 0.9 copy-start.6
  45.6 1.2 copy-start.2
  46.9 22.8 %copy-start.8 = (bf16[2,16,64,128]{3,2,1,0:T(8,128)(2,1)S(1)}, bf16[2,16,64,128]{3,2,1,0:T(8,128)(2,1)}, u32[]{:S(2)}) copy-start(bf16[2,16,64,128]{3,2,1,0:T(8,128)(2,1)} %get-tuple-element.15) | copy-start | bytes 1572868
  46.9 24.5 %copy-start.7 = (bf16[2,16,64,128]{3,2,1,0:T(8,128)(2,1)S(1)}, bf16[2,16,64,128]{3,2,1,0:T(8,128)(2,1)}, u32[]{:S(2)}) copy-start(bf16[2,16,64,128]{3,2,1,0:T(8,128)(2,1)} %get-tuple-element.16) | copy-start | bytes 1572868
  59.2 10.2 %copy-start.9 = (bf16[2,16,64,128]{3,2,1,0:T(8,128)(2,1)S(1)}, bf16[2,16,64,128]{3,2,1,0:T(8,128)(2,1)}, u32[]{:S(2)}) copy-start(bf16[2,16,64,128]{3,2,1,0:T(8,128)(2,1)} %get-tuple-element.14) | copy-start | bytes 1572868
  59.2 59.9 %all-to-all-start.2 = ((s16[32,136,128]{2,1,0:T(8,128)(2,1)}), s16[32,136,128]{2,1,0:T(8,128)(2,1)S(1)}, u32[]{:S(2)}, u32[]{:S(2)}) async-start(s16[32,136,128]{2,1,0:T(8,128)(2,1)} %bitcast.50), calls=%async_computation.2 | async-start | bytes 2228224 | tf_op jit(solution)/shard_map/all_to_all | solution.py:448
  69.4 23.9 %collective-permute-start.4 = (bf16[2,16,64,128]{3,2,1,0:T(8,128)(2,1)S(1)}, bf16[2,16,64,128]{3,2,1,0:T(8,128)(2,1)S(1)}, u32[]{:S(2)}, u32[]{:S(2)}) collective-permute-start(bf16[2,16,64,128]{3,2,1,0:T(8,128)(2,1)S(1)} %copy-done.9), channel_id=1, source_target_pairs={{0,8},{8,16},{16,24},{24,0},{1,9},{9,17},{17,25},{25,1},{2,10},{10... | collective-permute-start | bytes 1572872 | tf_op jit(solution)/shard_map/ppermute | solution.py:406
  69.7 24.9 %collective-permute-start.5 = (bf16[2,16,64,128]{3,2,1,0:T(8,128)(2,1)S(1)}, bf16[2,16,64,128]{3,2,1,0:T(8,128)(2,1)S(1)}, u32[]{:S(2)}, u32[]{:S(2)}) collective-permute-start(bf16[2,16,64,128]{3,2,1,0:T(8,128)(2,1)S(1)} %copy-done.8), channel_id=1, source_target_pairs={{0,16},{8,24},{16,0},{24,8},{1,17},{9,25},{17,1},{25,9},{2,18},{10... | collective-permute-start | bytes 1572872 | tf_op jit(solution)/shard_map/ppermute | solution.py:406
  71.3 33.2 %collective-permute-start.6 = (bf16[2,16,64,128]{3,2,1,0:T(8,128)(2,1)S(1)}, bf16[2,16,64,128]{3,2,1,0:T(8,128)(2,1)S(1)}, u32[]{:S(2)}, u32[]{:S(2)}) collective-permute-start(bf16[2,16,64,128]{3,2,1,0:T(8,128)(2,1)S(1)} %copy-done.7), channel_id=1, source_target_pairs={{0,24},{8,0},{16,8},{24,16},{1,25},{9,1},{17,9},{25,17},{2,26},{10... | collective-permute-start | bytes 1572872 | tf_op jit(solution)/shard_map/ppermute | solution.py:406
  93.3 12.0 %copy-start.10 = (bf16[2,16,64,128]{3,2,1,0:T(8,128)(2,1)}, bf16[2,16,64,128]{3,2,1,0:T(8,128)(2,1)S(1)}, u32[]{:S(2)}) copy-start(bf16[2,16,64,128]{3,2,1,0:T(8,128)(2,1)S(1)} %collective-permute-done.4) | copy-start | bytes 1572868
  94.6 10.0 %copy-start.11 = (bf16[2,16,64,128]{3,2,1,0:T(8,128)(2,1)}, bf16[2,16,64,128]{3,2,1,0:T(8,128)(2,1)S(1)}, u32[]{:S(2)}) copy-start(bf16[2,16,64,128]{3,2,1,0:T(8,128)(2,1)S(1)} %collective-permute-done.5) | copy-start | bytes 1572868
  104.5 0.8 copy-start.12
  119.1 1.0 copy-start.1
  119.1 7.6 %copy-start.14 = (pred[4,8,8]{2,1,0:T(8,128)(4,1)S(1)}, pred[4,8,8]{2,1,0:T(8,128)(4,1)}, u32[]{:S(2)}) copy-start(pred[4,8,8]{2,1,0:T(8,128)(4,1)} %get-tuple-element.19) | copy-start | bytes 772
  120.1 57.9 %all-to-all-start = ((s16[32,264,128]{2,1,0:T(8,128)(2,1)}), s16[32,264,128]{2,1,0:T(8,128)(2,1)S(1)}, u32[]{:S(2)}, u32[]{:S(2)}) async-start(s16[32,264,128]{2,1,0:T(8,128)(2,1)} %bitcast.49), calls=%async_computation | async-start | bytes 4325376 | tf_op jit(solution)/shard_map/all_to_all | solution.py:448
  178.1 1.4 copy-start

commit v2 on v1

--- a/solution.py
+++ b/solution.py
@@ -101,8 +101,7 @@
     exponent = code_exponent(values)
     code = jnp.round(values * (1.0 / code_scale(exponent))[None])
     code_ref[0, :members, :] = code.astype(jnp.int32).reshape(members, members).astype(jnp.int16)
-    tail = jnp.concatenate([exponent, exponent], axis=0).astype(jnp.int32)
-    code_ref[0, members:, :] = tail.astype(jnp.int16)
+    code_ref[0, members:, :] = exponent.astype(jnp.int32).astype(jnp.int16)
 
 
 def coded_transforms(obs_ensemble, obs_value, obs_weight, fill):
@@ -122,10 +121,10 @@
                 pl.BlockSpec((1, 1, width, observations), lambda n, h: (h[0], n, 0, 0)),
             ]
             + [pl.BlockSpec((1, width, observations), lambda n, h: (n, 0, 0))] * len(arrived),
-            out_specs=pl.BlockSpec((1, members + 16, members), lambda n, h: (n, 0, 0)),
+            out_specs=pl.BlockSpec((1, members + 8, members), lambda n, h: (n, 0, 0)),
             scratch_shapes=[pltpu.VMEM((members, observations), jnp.float32)],
         ),
-        out_shape=jax.ShapeDtypeStruct((points, members + 16, members), jnp.int16),
+        out_shape=jax.ShapeDtypeStruct((points, members + 8, members), jnp.int16),
         name="transforms",
     )(here, obs_value[:, None], obs_weight[:, None], obs_ensemble, *arrived)
 
@@ -201,7 +200,7 @@
             tiles = side_ref.shape[0]
             for n in range(tiles):
                 tail = side_ref[n, members:, :].astype(jnp.int32).astype(jnp.float32)
-                scale = code_scale(tail[:8])[None]
+                scale = code_scale(tail)[None]
 
                 def decode(r, carry):
                     start = pl.multiple_of(r * 64, 64)
@@ -210,7 +209,7 @@
                     table_ref[side * tiles + n, pl.ds(start, 64), :] = value.reshape(64, members)
                     return carry
 
-                lax.fori_loop(0, members // 64, decode, 0)
+                lax.fori_loop(0, members // 64, decode, 0, unroll=True)
 
     first_column = from_ref[owner] * block_size
     width = members // member_count
@@ -395,6 +394,9 @@
     order = (band_index + jnp.arange(member_count, dtype=jnp.int32)) % member_count
     early, late = pack_lanes(background[:, 0].transpose(0, 2, 3, 1), order, cut)
     early = lax.all_to_all(early, "member", split_axis=0, concat_axis=0, tiled=True)
+    late, block_target, stencil, stencil_weight, coded = lax.optimization_barrier(
+        (late, block_target, stencil, stencil_weight, coded)
+    )
     late = [late[step] for step in range(member_count)]
     left, right = halo_pair(coded, "region")
     left, *late = lax.optimization_barrier((left, *late))

time: 186 us -> 182 us (0.978)
  waiting for transfers between devices: 82.2 us -> 80 us
    ppermute x2, waiting for transfers between devices: 3.93 us -> 1.79 us  [halo_pair(): lax.ppermute(block, axis, forward)]
    unnamed x30 -> x34, local copies, waits for them, and re-layouts: 4.44 us -> 4.41 us
  transfers between devices with their start and end apart: 13 -> 13, of which waited for: 5 -> 5; matrix products, arithmetic and copies ran while one was open for 5% -> 4% of each run, Pallas kernels for 17% -> 18%
where the time goes in v2:
time: 182 us; the launch traced here: 181 us
  waiting for transfers between devices  80 us (44%)
  Pallas kernels  49.3 us (27%)
  starting transfers between devices  38.9 us (21%)
  local copies, waits for them, and re-layouts  6.83 us (4%)
  other arithmetic  5.79 us (3%)
    all_to_all x2, waiting for transfers between devices, analysis_shards(): lax.all_to_all(outgoing, ('member', 'region'), split_axis=0, concat_axis=...  46.9 us
    ppermute x3, waiting for transfers between devices, analysis_shards(): arrived = lax.ppermute(late[step], 'member', ring)  31.3 us
    pallas_call x2, Pallas kernels, columns_to_blocks(): pl.pallas_call(kernel, grid_spec=pltpu.PrefetchScalarGridSpec(num_scalar_...  25.7 us
    all_to_all x2, starting transfers between devices, analysis_shards(): lax.all_to_all(outgoing, ('member', 'region'), split_axis=0, concat_axis=...  17 us
    pallas_call x2, Pallas kernels, blocks_to_native(): pl.pallas_call(functools.partial(native_kernel, places=places, block_size...  9.05 us
    pallas_call x1, Pallas kernels, coded_transforms(): pl.pallas_call(functools.partial(transform_kernel, member_count=member_co...  8.14 us
    ppermute x2, starting transfers between devices, halo_pair(): lax.ppermute(block, axis, forward)  7.61 us
    pallas_call x1, Pallas kernels, pack_lanes(): pl.pallas_call(functools.partial(pack_kernel, group=group), grid_spec=plt...  6.39 us
  transfers between devices with their start and end apart: 13, of which 5 were waited for; matrix products, arithmetic and copies ran while one was open for 4% of the time, Pallas kernels for 18%

profile of v2, /device:TPU:0, one launch (start us, length us, event | category | flops | bytes accessed | tf_op | source)
XLA Modules:
  0.0 181.1 jit_solution(17732281275945943379)
XLA Ops:
  0.0 1.1 dynamic-slice_bitcast_fusion
  1.1 0.5 collective-permute-start.2
  1.6 2.0 %collective-permute-start = (bf16[1,64,1024]{2,1,0:T(8,128)(2,1)S(1)}, bf16[1,64,1024]{2,1,0:T(8,128)(2,1)}, u32[]{:S(2)}, u32[]{:S(2)}) collective-permute-start(bf16[1,64,1024]{2,1,0:T(8,128)(2,1)S(1)} %get-tuple-element.36), channel_id=1, source_target_pairs={{0,24},{8,0},{16,8},{24,16},{1,25},{9,1},{17,9},{25,17},{2,26},{10... | collective-permute-start | bytes 393224 | tf_op jit(solution)/shard_map/ppermute | solution.py:31
  3.6 2.2 %collective-permute-start.1 = (bf16[1,64,1024]{2,1,0:T(8,128)(2,1)S(1)}, bf16[1,64,1024]{2,1,0:T(8,128)(2,1)}, u32[]{:S(2)}, u32[]{:S(2)}) collective-permute-start(bf16[1,64,1024]{2,1,0:T(8,128)(2,1)S(1)} %get-tuple-element.37), channel_id=1, source_target_pairs={{0,16},{8,24},{16,0},{24,8},{1,17},{9,25},{17,1},{25,9},{2,18},{10... | collective-permute-start | bytes 393224 | tf_op jit(solution)/shard_map/ppermute | solution.py:31
  5.8 0.6 and_select_fusion.1.order_ref
  6.4 6.4 %pack.1 = (bf16[4,1,16,64,128]{4,3,2,1,0:T(8,128)(2,1)}, bf16[4,2,16,64,128]{4,3,2,1,0:T(8,128)(2,1)}) custom-call(s32[4]{0:T(128)} %and_select_fusion.1.order_ref, bf16[4,64,64,96]{3,2,1,0:T(8,128)(2,1)} %bitcast.51), custom_call_target="tpu_custom_call" | custom-call | tf_op jit(solution)/shard_map/pack/pallas_call | solution.py:173
  12.8 3.6 %all-to-all-start.1 = ((bf16[4,1,16,64,128]{4,3,2,1,0:T(8,128)(2,1)}), bf16[4,1,16,64,128]{4,3,2,1,0:T(8,128)(2,1)S(1)}, u32[]{:S(2)}, u32[]{:S(2)}) async-start(bf16[4,1,16,64,128]{4,3,2,1,0:T(8,128)(2,1)} %get-tuple-element.28), calls=%async_computation.1 | async-start | bytes 2097152 | tf_op jit(solution)/shard_map/all_to_all | solution.py:396
  16.5 0.0 collective-permute-done.2.refs_2_
  16.5 0.0 collective-permute-done.refs_0_
  16.5 0.0 collective-permute-done.1.refs_1_
  16.5 8.1 %transforms.1 = s16[1,264,256]{2,1,0:T(8,128)(2,1)} custom-call(s32[1]{0:T(128)} %bitcast.2.here_ref, f32[1,1,1024]{2,1,0:T(1,128)} %bitcast.58, f32[1,1,1024]{2,1,0:T(1,128)} %bitcast.59, bf16[4,1,64,1024]{3,2,1,0:T(8,128)(2,1)} %bitcast.54, bf16[1,64,1024]{2,1,0:T(8,128)(2,1)} %collective-permute-done.refs_0_, ...), custom_call_target="tpu_custom_call" | custom-call | tf_op jit(solution)/shard_map/transforms/pallas_call | solution.py:113
  24.6 1.3 collective-permute-start.7
  25.9 4.6 %collective-permute-start.3 = (s16[1,264,256]{2,1,0:T(8,128)(2,1)}, s16[1,264,256]{2,1,0:T(8,128)(2,1)S(1)}, u32[]{:S(2)}, u32[]{:S(2)}) collective-permute-start(s16[1,264,256]{2,1,0:T(8,128)(2,1)} %transforms.1), channel_id=1, source_target_pairs={{0,1},{1,2},{2,3},{3,4},{4,5},{5,6},{6,7},{8,9},{9,10},{10,11},{11... | collective-permute-start | bytes 405512 | tf_op jit(solution)/shard_map/ppermute | solution.py:21
  30.5 0.0 copy-done.12
  30.5 0.6 broadcast_compare_fusion
  31.1 0.0 copy-done.4
  31.1 1.3 slice_bitcast_fusion
  32.5 0.7 reduce_sum.29
  33.2 0.6 select_reduce_fusion.1.from_ref
  33.8 1.8 collective-permute-done.3
  35.6 0.0 copy-done.7
  35.6 0.0 collective-permute-done.7
  35.7 0.0 copy-start.3
  35.7 1.3 collective-permute-start.9
  37.0 3.1 %collective-permute-start.8 = (s16[3,264,256]{2,1,0:T(8,128)(2,1)S(1)}, s16[3,264,256]{2,1,0:T(8,128)(2,1)S(1)}, u32[]{:S(2)}, u32[]{:S(2)}) collective-permute-start(s16[3,264,256]{2,1,0:T(8,128)(2,1)S(1)} %constant_dynamic-update-slice_fusion.refs_5_.refs_2_), channel_id=1, source_target_pairs={{0,8},{8,16},{16,24},{1,9},{9,17},{17,25},{2,10},{10,18},{18,26},{... | collective-permute-start | bytes 1216520 | tf_op jit(solution)/shard_map/ppermute | solution.py:21
  40.0 1.3 fusion.6.slot_ref
  41.3 0.0 copy-done.15
  41.3 0.6 bitcast_divide_fusion.share_ref
  41.9 0.0 collective-permute-done.9.refs_6_.refs_3_
  41.9 0.0 collective-permute-done.8.refs_4_.refs_1_
  41.9 0.0 copy-start.6
  41.9 0.0 all-to-all-done.1
  42.0 0.0 copy-start.2
  42.0 0.0 copy-done.3
  42.0 0.8 copy-done.5
  42.7 0.1 copy-done.6
  42.9 0.3 copy-done.2
  43.2 12.1 %columns.3 = s16[4,8,136,128]{3,2,1,0:T(8,128)(2,1)} custom-call(s32[8]{0:T(128)} %select_reduce_fusion.1.from_ref, s32[4,64]{1,0:T(4,128)} %fusion.6.slot_ref, f32[4,64]{1,0:T(4,128)} %bitcast_divide_fusion.share_ref, s32[1]{0:T(128)} %constant.157.clone.1.source_ref, bf16[64,64,128]{2,1,0:T(8,128)(2,1)} %bitcast.52, s16[3,264,256]{2,1,0:T(8,128)(2,1)} %copy-done.6, ...), custom_call_target="tpu_custom_call" | custom-call | flops 536870912 | bytes 2097152 | tf_op jit(solution)/shard_map/columns/pallas_call | solution.py:294
  55.3 10.8 %all-to-all-start.2 = ((s16[32,136,128]{2,1,0:T(8,128)(2,1)}), s16[32,136,128]{2,1,0:T(8,128)(2,1)S(1)}, u32[]{:S(2)}, u32[]{:S(2)}) async-start(s16[32,136,128]{2,1,0:T(8,128)(2,1)} %bitcast.50), calls=%async_computation.2 | async-start | bytes 2228224 | tf_op jit(solution)/shard_map/all_to_all | solution.py:450
  66.2 0.3 collective-permute-start.4
  66.5 1.6 collective-permute-start.5
  68.1 0.0 copy-done.11
  68.1 1.4 collective-permute-start.6
  69.5 0.6 and_select_fusion.source_ref
  70.0 20.1 %collective-permute-done.4 = bf16[2,16,64,128]{3,2,1,0:T(8,128)(2,1)S(1)} collective-permute-done((bf16[2,16,64,128]{3,2,1,0:T(8,128)(2,1)}, bf16[2,16,64,128]{3,2,1,0:T(8,128)(2,1)S(1)}, u32[]{:S(2)}, u32[]{:S(2)}) %collective-permute-start.4) | collective-permute-done | bytes 524320 | tf_op jit(solution)/shard_map/ppermute | solution.py:408
  90.1 1.3 collective-permute-done.5
  91.4 9.9 %collective-permute-done.6 = bf16[2,16,64,128]{3,2,1,0:T(8,128)(2,1)S(1)} collective-permute-done((bf16[2,16,64,128]{3,2,1,0:T(8,128)(2,1)S(1)}, bf16[2,16,64,128]{3,2,1,0:T(8,128)(2,1)S(1)}, u32[]{:S(2)}, u32[]{:S(2)}) %collective-permute-start.6) | collective-permute-done | bytes 524320 | tf_op jit(solution)/shard_map/ppermute | solution.py:408
  101.3 0.0 copy-done.8
  101.3 0.0 copy-done.9
  101.3 0.8 copy-done.10
  102.1 13.6 %columns.2 = s16[4,8,264,128]{3,2,1,0:T(8,128)(2,1)} custom-call(s32[8]{0:T(128)} %select_reduce_fusion.1.from_ref, s32[4,64]{1,0:T(4,128)} %fusion.6.slot_ref, f32[4,64]{1,0:T(4,128)} %bitcast_divide_fusion.share_ref, s32[4]{0:T(128)} %and_select_fusion.source_ref, bf16[32,64,128]{2,1,0:T(8,128)(2,1)} %bitcast.53, bf16[32,64,128]{2,1,0:T(8,128)(2,1)} %bitcast.55, ...), custom_call_target="tpu_custom_call" | custom-call | flops 1073741824 | bytes 4194304 | tf_op jit(solution)/shard_map/columns/pallas_call | solution.py:294
  115.7 0.0 all-to-all-done.2.code_ref
  115.7 0.0 copy-start.13
  115.7 0.0 copy-start.14
  115.7 1.0 copy-done.1
  116.7 6.1 %all-to-all-start = ((s16[32,264,128]{2,1,0:T(8,128)(2,1)}), s16[32,264,128]{2,1,0:T(8,128)(2,1)S(1)}, u32[]{:S(2)}, u32[]{:S(2)}) async-start(s16[32,264,128]{2,1,0:T(8,128)(2,1)} %bitcast.49), calls=%async_computation | async-start | bytes 4325376 | tf_op jit(solution)/shard_map/all_to_all | solution.py:450
  122.9 0.1 iota_add_fusion
  122.9 0.0 copy-done.13
  123.0 0.0 copy-done.14
  123.0 0.8 select_reduce_fusion.source_ref
  123.7 3.7 %native.2.refs_0_ = f32[96,64,256]{2,1,0:T(8,128)} custom-call(s32[32]{0:T(128)} %select_reduce_fusion.source_ref, s16[32,136,128]{2,1,0:T(8,128)(2,1)} %copy-done.1), custom_call_target="tpu_custom_call" | custom-call | tf_op jit(solution)/shard_map/native/pallas_call | solution.py:363
  127.4 46.9 %all-to-all-done.code_ref = s16[32,264,128]{2,1,0:T(8,128)(2,1)S(1)} async-done(((s16[32,264,128]{2,1,0:T(8,128)(2,1)}), s16[32,264,128]{2,1,0:T(8,128)(2,1)S(1)}, u32[]{:S(2)}, u32[]{:S(2)}) %all-to-all-start) | async-done | bytes 2162720 | tf_op jit(solution)/shard_map/all_to_all | solution.py:450
  174.3 1.4 copy-done
  175.7 5.4 %native.3 = f32[96,64,256]{2,1,0:T(8,128)} custom-call(s32[32]{0:T(128)} %select_reduce_fusion.source_ref, s16[32,264,128]{2,1,0:T(8,128)(2,1)} %copy-done, f32[96,64,256]{2,1,0:T(8,128)} %native.2.refs_0_), custom_call_target="tpu_custom_call", output_to_operand_aliasing={{}: (2, {})} | custom-call | tf_op jit(solution)/shard_map/native/pallas_call | solution.py:363
  (17 shorter events, 0.1 us)
Async XLA Ops:
  1.1 15.4 %collective-permute-start.2 = (bf16[1,64,1024]{2,1,0:T(8,128)(2,1)S(1)}, bf16[1,64,1024]{2,1,0:T(8,128)(2,1)}, u32[]{:S(2)}, u32[]{:S(2)}) collective-permute-start(bf16[1,64,1024]{2,1,0:T(8,128)(2,1)S(1)} %get-tuple-element.35), channel_id=1, source_target_pairs={{0,8},{8,16},{16,24},{24,0},{1,9},{9,17},{17,25},{25,1},{2,10},{10... | collective-permute-start | bytes 393224 | tf_op jit(solution)/shard_map/ppermute | solution.py:31
  1.6 14.9 %collective-permute-start = (bf16[1,64,1024]{2,1,0:T(8,128)(2,1)S(1)}, bf16[1,64,1024]{2,1,0:T(8,128)(2,1)}, u32[]{:S(2)}, u32[]{:S(2)}) collective-permute-start(bf16[1,64,1024]{2,1,0:T(8,128)(2,1)S(1)} %get-tuple-element.36), channel_id=1, source_target_pairs={{0,24},{8,0},{16,8},{24,16},{1,25},{9,1},{17,9},{25,17},{2,26},{10... | collective-permute-start | bytes 393224 | tf_op jit(solution)/shard_map/ppermute | solution.py:31
  3.6 12.9 %collective-permute-start.1 = (bf16[1,64,1024]{2,1,0:T(8,128)(2,1)S(1)}, bf16[1,64,1024]{2,1,0:T(8,128)(2,1)}, u32[]{:S(2)}, u32[]{:S(2)}) collective-permute-start(bf16[1,64,1024]{2,1,0:T(8,128)(2,1)S(1)} %get-tuple-element.37), channel_id=1, source_target_pairs={{0,16},{8,24},{16,0},{24,8},{1,17},{9,25},{17,1},{25,9},{2,18},{10... | collective-permute-start | bytes 393224 | tf_op jit(solution)/shard_map/ppermute | solution.py:31
  12.8 17.7 %copy-start.12 = (s32[4,8,8]{2,1,0:T(8,128)S(1)}, s32[4,8,8]{2,1,0:T(8,128)}, u32[]{:S(2)}) copy-start(s32[4,8,8]{2,1,0:T(8,128)} %param.13) | copy-start | bytes 3076
  12.8 18.3 %copy-start.4 = (bf16[4,2,16,64,128]{4,3,2,1,0:T(8,128)(2,1)S(1)}, bf16[4,2,16,64,128]{4,3,2,1,0:T(8,128)(2,1)}, u32[]{:S(2)}) copy-start(bf16[4,2,16,64,128]{4,3,2,1,0:T(8,128)(2,1)} %get-tuple-element.22) | copy-start | bytes 6291460
  12.8 29.1 %all-to-all-start.1 = ((bf16[4,1,16,64,128]{4,3,2,1,0:T(8,128)(2,1)}), bf16[4,1,16,64,128]{4,3,2,1,0:T(8,128)(2,1)S(1)}, u32[]{:S(2)}, u32[]{:S(2)}) async-start(bf16[4,1,16,64,128]{4,3,2,1,0:T(8,128)(2,1)} %get-tuple-element.28), calls=%async_computation.1 | async-start | bytes 2097152 | tf_op jit(solution)/shard_map/all_to_all | solution.py:396
  24.6 11.0 %collective-permute-start.7 = (s16[1,264,256]{2,1,0:T(8,128)(2,1)}, s16[1,264,256]{2,1,0:T(8,128)(2,1)S(1)}, u32[]{:S(2)}, u32[]{:S(2)}) collective-permute-start(s16[1,264,256]{2,1,0:T(8,128)(2,1)} %transforms.1), channel_id=1, source_target_pairs={{1,0},{2,1},{3,2},{4,3},{5,4},{6,5},{7,6},{9,8},{10,9},{11,10},{12... | collective-permute-start | bytes 405512 | tf_op jit(solution)/shard_map/ppermute | solution.py:21
  25.9 9.7 %collective-permute-start.3 = (s16[1,264,256]{2,1,0:T(8,128)(2,1)}, s16[1,264,256]{2,1,0:T(8,128)(2,1)S(1)}, u32[]{:S(2)}, u32[]{:S(2)}) collective-permute-start(s16[1,264,256]{2,1,0:T(8,128)(2,1)} %transforms.1), channel_id=1, source_target_pairs={{0,1},{1,2},{2,3},{3,4},{4,5},{5,6},{6,7},{8,9},{9,10},{10,11},{11... | collective-permute-start | bytes 405512 | tf_op jit(solution)/shard_map/ppermute | solution.py:21
  31.1 4.5 %copy-start.7 = (s16[1,264,256]{2,1,0:T(8,128)(2,1)S(1)}, s16[1,264,256]{2,1,0:T(8,128)(2,1)}, u32[]{:S(2)}) copy-start(s16[1,264,256]{2,1,0:T(8,128)(2,1)} %transforms.1) | copy-start | bytes 405508
  31.1 10.2 %copy-start.15 = (f32[1,1,4,64]{3,2,1,0:T(4,128)S(1)}, f32[1,1,4,64]{3,2,1,0:T(4,128)}, u32[]{:S(2)}) copy-start(f32[1,1,4,64]{3,2,1,0:T(4,128)} %param.12) | copy-start | bytes 3076
  35.7 6.3 %copy-start.3 = (s16[3,264,256]{2,1,0:T(8,128)(2,1)}, s16[3,264,256]{2,1,0:T(8,128)(2,1)S(1)}, u32[]{:S(2)}) copy-start(s16[3,264,256]{2,1,0:T(8,128)(2,1)S(1)} %constant_dynamic-update-slice_fusion.refs_5_.refs_2_) | copy-start | bytes 1216516
  35.7 6.2 %collective-permute-start.9 = (s16[3,264,256]{2,1,0:T(8,128)(2,1)S(1)}, s16[3,264,256]{2,1,0:T(8,128)(2,1)S(1)}, u32[]{:S(2)}, u32[]{:S(2)}) collective-permute-start(s16[3,264,256]{2,1,0:T(8,128)(2,1)S(1)} %constant_dynamic-update-slice_fusion.refs_5_.refs_2_), channel_id=1, source_target_pairs={{8,0},{16,8},{24,16},{9,1},{17,9},{25,17},{10,2},{18,10},{26,18},{... | collective-permute-start | bytes 1216520 | tf_op jit(solution)/shard_map/ppermute | solution.py:21
  37.0 4.9 %collective-permute-start.8 = (s16[3,264,256]{2,1,0:T(8,128)(2,1)S(1)}, s16[3,264,256]{2,1,0:T(8,128)(2,1)S(1)}, u32[]{:S(2)}, u32[]{:S(2)}) collective-permute-start(s16[3,264,256]{2,1,0:T(8,128)(2,1)S(1)} %constant_dynamic-update-slice_fusion.refs_5_.refs_2_), channel_id=1, source_target_pairs={{0,8},{8,16},{16,24},{1,9},{9,17},{17,25},{2,10},{10,18},{18,26},{... | collective-permute-start | bytes 1216520 | tf_op jit(solution)/shard_map/ppermute | solution.py:21
  41.9 0.8 copy-start.5
  41.9 0.9 copy-start.6
  42.0 1.2 copy-start.2
  43.2 24.9 %copy-start.11 = (bf16[2,16,64,128]{3,2,1,0:T(8,128)(2,1)S(1)}, bf16[2,16,64,128]{3,2,1,0:T(8,128)(2,1)}, u32[]{:S(2)}) copy-start(bf16[2,16,64,128]{3,2,1,0:T(8,128)(2,1)} %get-tuple-element.26) | copy-start | bytes 1572868
  55.3 60.4 %all-to-all-start.2 = ((s16[32,136,128]{2,1,0:T(8,128)(2,1)}), s16[32,136,128]{2,1,0:T(8,128)(2,1)S(1)}, u32[]{:S(2)}, u32[]{:S(2)}) async-start(s16[32,136,128]{2,1,0:T(8,128)(2,1)} %bitcast.50), calls=%async_computation.2 | async-start | bytes 2228224 | tf_op jit(solution)/shard_map/all_to_all | solution.py:450
  66.2 23.9 %collective-permute-start.4 = (bf16[2,16,64,128]{3,2,1,0:T(8,128)(2,1)}, bf16[2,16,64,128]{3,2,1,0:T(8,128)(2,1)S(1)}, u32[]{:S(2)}, u32[]{:S(2)}) collective-permute-start(bf16[2,16,64,128]{3,2,1,0:T(8,128)(2,1)} %get-tuple-element.24), channel_id=1, source_target_pairs={{0,8},{8,16},{16,24},{24,0},{1,9},{9,17},{17,25},{25,1},{2,10},{10... | collective-permute-start | bytes 1572872 | tf_op jit(solution)/shard_map/ppermute | solution.py:408
  66.5 24.9 %collective-permute-start.5 = (bf16[2,16,64,128]{3,2,1,0:T(8,128)(2,1)}, bf16[2,16,64,128]{3,2,1,0:T(8,128)(2,1)S(1)}, u32[]{:S(2)}, u32[]{:S(2)}) collective-permute-start(bf16[2,16,64,128]{3,2,1,0:T(8,128)(2,1)} %get-tuple-element.25), channel_id=1, source_target_pairs={{0,16},{8,24},{16,0},{24,8},{1,17},{9,25},{17,1},{25,9},{2,18},{10... | collective-permute-start | bytes 1572872 | tf_op jit(solution)/shard_map/ppermute | solution.py:408
  68.1 33.2 %collective-permute-start.6 = (bf16[2,16,64,128]{3,2,1,0:T(8,128)(2,1)S(1)}, bf16[2,16,64,128]{3,2,1,0:T(8,128)(2,1)S(1)}, u32[]{:S(2)}, u32[]{:S(2)}) collective-permute-start(bf16[2,16,64,128]{3,2,1,0:T(8,128)(2,1)S(1)} %copy-done.11), channel_id=1, source_target_pairs={{0,24},{8,0},{16,8},{24,16},{1,25},{9,1},{17,9},{25,17},{2,26},{10... | collective-permute-start | bytes 1572872 | tf_op jit(solution)/shard_map/ppermute | solution.py:408
  90.1 11.2 %copy-start.8 = (bf16[2,16,64,128]{3,2,1,0:T(8,128)(2,1)}, bf16[2,16,64,128]{3,2,1,0:T(8,128)(2,1)S(1)}, u32[]{:S(2)}) copy-start(bf16[2,16,64,128]{3,2,1,0:T(8,128)(2,1)S(1)} %collective-permute-done.4) | copy-start | bytes 1572868
  91.4 10.0 %copy-start.9 = (bf16[2,16,64,128]{3,2,1,0:T(8,128)(2,1)}, bf16[2,16,64,128]{3,2,1,0:T(8,128)(2,1)S(1)}, u32[]{:S(2)}) copy-start(bf16[2,16,64,128]{3,2,1,0:T(8,128)(2,1)S(1)} %collective-permute-done.5) | copy-start | bytes 1572868
  101.3 0.8 copy-start.10
  115.7 1.0 copy-start.1
  115.7 7.2 %copy-start.13 = (s32[4,8,8]{2,1,0:T(8,128)S(1)}, s32[4,8,8]{2,1,0:T(8,128)}, u32[]{:S(2)}) copy-start(s32[4,8,8]{2,1,0:T(8,128)} %param.13) | copy-start | bytes 3076
  115.7 7.3 %copy-start.14 = (pred[4,8,8]{2,1,0:T(8,128)(4,1)S(1)}, pred[4,8,8]{2,1,0:T(8,128)(4,1)}, u32[]{:S(2)}) copy-start(pred[4,8,8]{2,1,0:T(8,128)(4,1)} %get-tuple-element.29) | copy-start | bytes 772
  116.7 57.6 %all-to-all-start = ((s16[32,264,128]{2,1,0:T(8,128)(2,1)}), s16[32,264,128]{2,1,0:T(8,128)(2,1)S(1)}, u32[]{:S(2)}, u32[]{:S(2)}) async-start(s16[32,264,128]{2,1,0:T(8,128)(2,1)} %bitcast.49), calls=%async_computation | async-start | bytes 4325376 | tf_op jit(solution)/shard_map/all_to_all | solution.py:450
  174.3 1.4 copy-start
